TPU v7x, 32 devices: a whole 2x2x4 slice. The times are simulated.
32 devices in a mesh: groups: 2 (over x), kv: 16 (over z, y, core).
Axes of the slice: x: 2, y: 2, z: 4, core: 2. Of those that a mesh axis runs over, the one named last changes fastest.
Arguments:
- queries: bfloat16 [80, 18432], P('groups', 'kv'), parts along dimension 0, may hold values from -240 to 240
- latent_cache: bfloat16 [80, 2048, 576], P('groups', 'kv'), parts along dimension 0, may hold values from -6 to 6
- context_lengths: int32 [80], P('groups'), parts along dimension 0, may hold values from 128 to 2048, as said below
- value_up: bfloat16 [16384, 128], P('kv'), may hold values from -0.25 to 0.25
- out_proj: bfloat16 [4096, 7168], P('kv'), may hold values from -0.09375 to 0.09375
- residual: bfloat16 [80, 7168], P('groups', 'kv'), parts along dimension 0, may hold values from -0.75 to 0.75
- norm_gain: bfloat16 [7168], P('kv'), may hold values from 0.5 to 1.5
- expert_ids: int32 [80, 8], P('groups'), parts along dimension 0, may hold values from 0 to 255, all different within a row; in each aligned block of 40 rows (0 to 39, 40 to 79, ...) at most 2 rows name the same one
- gate_weights: float32 [80, 8], P('groups'), parts along dimension 0, may hold values from 0.05 to 0.5
Outputs:
- dispatched: bfloat16 [512, 2, 7168], P(('groups', 'kv')), parts along dimension 0
- slot_scale: float32 [512, 2], P(('groups', 'kv')), parts along dimension 0
- slot_gate: float32 [512, 2], P(('groups', 'kv')), parts along dimension 0
There are 2 independent parts, one for each index of `groups`. A program takes and returns all parts, laid end to end along the dimension named above; an argument that names none is the same for every part. Nothing has to cross between parts.
Inputs may be any that keep to these rules, and one draw needn't show every extreme that they name: `context_lengths`: multiples of 128; some sequence is 2048 long. `expert_ids`: each token names 8 different experts; no expert is named by more than 2 tokens, a bound that some block reaches.
All inputs are finite; a program needn't handle non-finite values. Where the computation divides by a largest or mean magnitude, that divisor is 1e-20 or more.
Results may differ from a plain program's by a relative error of at most 0.0069.
Values may be sent and summed in bfloat16 or wider, within the bound.
A program may use at most 64 MiB of HBM per device.

v0:
```python
import jax
import jax.numpy as jnp
from jax import lax
from jax.sharding import PartitionSpec as P

H = 32
LAT = 512
ROPE = 64
VD = 128
D = 7168
EXPERTS = 256
TOPK = 8
CAP = 2


score_scale = 192.0 ** (-0.5)
masked_score = -1e30
small_eps = 1e-06


def from_partner(value, axis, bit):
    mask = 2**bit
    pairs = [(source, source ^ mask) for source in range(lax.axis_size(axis))]
    return lax.ppermute(value, axis, pairs)


def slot_targets(expert_ids):
    flat_ids = expert_ids.reshape(-1)
    order_index = jnp.arange(flat_ids.shape[0], dtype=jnp.int32)
    same_before = (flat_ids[:, None] == flat_ids[None, :]) & (
        order_index[None, :] < order_index[:, None]
    )
    rank_within = jnp.sum(same_before.astype(jnp.int32), axis=1)
    return flat_ids * CAP + rank_within


def slot_match(targets, first_slot, slot_count):
    slot_index = first_slot + jnp.arange(slot_count, dtype=jnp.int32)
    return (slot_index[:, None] == targets[None, :]).astype(jnp.float32)


def token_picker(matches, seq_count):
    return jnp.sum(matches.reshape(matches.shape[0], seq_count, TOPK), axis=2)


def per_device(
    queries,
    latent_cache,
    context_lengths,
    value_up,
    out_proj,
    residual,
    norm_gain,
    expert_ids,
    gate_weights,
):
    kv_count = lax.axis_size("kv")
    shard_index = lax.axis_index("kv")
    seq_count = queries.shape[0]
    query_rows = lax.all_gather(queries, "kv", axis=1, tiled=True).reshape(seq_count, H, LAT + ROPE)
    ctx_local = latent_cache.shape[1]
    scores = (
        jnp.einsum("shq,scq->shc", query_rows, latent_cache, preferred_element_type=jnp.float32)
        * score_scale
    )
    position = shard_index * ctx_local + jnp.arange(ctx_local, dtype=jnp.int32)
    valid_mask = (position[None, :] < context_lengths[:, None])[:, None, :]
    scores = jnp.where(valid_mask, scores, masked_score)
    local_max = jnp.max(scores, axis=2)
    weights = jnp.where(valid_mask, jnp.exp(scores - local_max[:, :, None]), 0.0)
    local_total = jnp.sum(weights, axis=2)
    local_out = jnp.einsum(
        "shc,scl->shl",
        weights.astype(jnp.bfloat16),
        latent_cache[:, :, :LAT],
        preferred_element_type=jnp.float32,
    )
    out_rows = out_proj.shape[0]
    col_count = H * LAT // kv_count
    segment = min(col_count, LAT)
    head_count = col_count // segment
    head_start = shard_index * col_count // LAT
    global_max = lax.pmax(local_max, "kv")
    scaling = jnp.exp(local_max - global_max)
    weight_total = lax.psum(local_total * scaling, "kv")
    scaled = (local_out * scaling[:, :, None]).reshape(seq_count, H * LAT)
    merged_sum = lax.psum_scatter(scaled, "kv", scatter_dimension=1, tiled=True).reshape(
        seq_count, head_count, segment
    )
    own_total = lax.dynamic_slice_in_dim(weight_total, head_start, head_count, 1)
    merged = merged_sum / own_total[:, :, None]
    projector = value_up.reshape(head_count, segment, VD).astype(jnp.float32)
    value_part = jnp.einsum("shl,hlv->shv", merged, projector, precision=lax.Precision.HIGHEST)
    holders = kv_count // H if kv_count > H else 1
    for bit in range(holders.bit_length() - 1):
        value_part = value_part + from_partner(value_part, "kv", bit)
    value_rows = value_part.astype(jnp.bfloat16).reshape(seq_count, head_count * VD)
    if holders > 1:
        value_rows = lax.dynamic_slice_in_dim(
            value_rows, shard_index % holders * out_rows, out_rows, 1
        )
    partial_out = jnp.dot(value_rows, out_proj, preferred_element_type=jnp.float32)
    experts_local = EXPERTS // kv_count
    slot_count = experts_local * CAP
    targets = slot_targets(expert_ids)
    own_match = slot_match(targets, shard_index * slot_count, slot_count)
    own_pick = token_picker(own_match, seq_count)
    slot_gate = jnp.dot(own_match, gate_weights.reshape(-1), precision=lax.Precision.HIGHEST)
    attn_rows = lax.psum(partial_out, "kv")
    resid_rows, gain_cols = (
        lax.all_gather(residual, "kv", axis=1, tiled=True),
        lax.all_gather(norm_gain, "kv", axis=0, tiled=True),
    )
    summed = attn_rows + resid_rows.astype(jnp.float32)
    inverse_rms = lax.rsqrt(jnp.mean(summed * summed, axis=1) + small_eps)
    normed = summed * inverse_rms[:, None] * gain_cols.astype(jnp.float32)
    peak_abs = jnp.max(jnp.abs(normed), axis=1) + small_eps
    coded_rows = (normed / peak_abs[:, None]).astype(jnp.bfloat16)
    dispatched = jnp.dot(
        own_pick.astype(jnp.bfloat16), coded_rows, preferred_element_type=jnp.float32
    ).astype(jnp.bfloat16)
    slot_scale = jnp.dot(own_pick, peak_abs, precision=lax.Precision.HIGHEST)
    return (
        dispatched.reshape(experts_local, CAP, D),
        slot_scale.reshape(experts_local, CAP),
        slot_gate.reshape(experts_local, CAP),
    )


def solution(mesh):
    in_specs = (
        P("groups", "kv"),
        P("groups", "kv", None),
        P("groups"),
        P("kv", None),
        P("kv", None),
        P("groups", "kv"),
        P("kv"),
        P("groups", None),
        P("groups", None),
    )
    out_specs = (
        P(("groups", "kv"), None, None),
        P(("groups", "kv"), None),
        P(("groups", "kv"), None),
    )
    return jax.shard_map(
        per_device, mesh=mesh, in_specs=in_specs, out_specs=out_specs, check_vma=False
    )
```

profile of v0, /device:TPU:1, one launch (start us, length us, event | category | flops | bytes accessed | tf_op | source)
XLA Modules:
  0.0 312.8 jit_solution(11004834008479304627)
XLA Ops:
  7.2 0.7 all-gather.3.cloned.1.call-update
  8.0 0.7 broadcast_compare_fusion.1
  8.7 43.3 %all-gather.3.cloned.1.call-done = bf16[40,18432]{1,0:T(8,128)(2,1)} async-done(((bf16[40,1152]{1,0:T(8,128)(2,1)}), bf16[40,18432]{1,0:T(8,128)(2,1)}) %all-gather.3.cloned.1.call-update) | async-done | bytes 1474576 | tf_op jit(solution)/shard_map/all_gather | solution.py:60
  52.0 3.3 %reshape.111 = bf16[40,32,576]{2,1,0:T(8,128)(2,1)S(1)} reshape(bf16[40,18432]{1,0:T(8,128)(2,1)} %all-gather.3.cloned.1.call-done) | data formatting | bytes 2949120 | tf_op jit(solution)/shard_map/reshape | solution.py:60
  55.3 3.9 %fusion.26 = (f32[40,32]{1,0:T(8,128)S(1)}, f32[40,32,128]{2,1,0:T(8,128)S(1)}) fusion(bf16[40,32,576]{2,1,0:T(8,128)(2,1)S(1)} %reshape.111, bf16[40,128,576]{1,2,0:T(8,128)(2,1)} %param.10, pred[40,128]{1,0:T(8,128)(4,1)S(1)} %broadcast_compare_fusion.1), kind=kOutput, calls=%fused_computation.47 | convolution fusion | flops 189233920 | bytes 8038400 | tf_op jit(solution)/shard_map/shq,scq->shc/dot_general | solution.py:63
  59.2 54.8 %pmax.7 = f32[40,32]{1,0:T(8,128)S(1)} all-reduce(f32[40,32]{1,0:T(8,128)S(1)} %get-tuple-element.5), channel_id=1, replica_groups=mesh['groups'=2,'kv'=16] {'kv'}, use_global_device_ids=true, to_apply=%region_3.4 | all-reduce | flops 1280 | bytes 10240 | tf_op jit(solution)/shard_map/pmax | solution.py:83
  113.9 0.4 fusion.7
  114.4 3.9 %fusion.2 = f32[40,32,512]{2,1,0:T(8,128)S(1)} fusion(bf16[40,128,576]{1,2,0:T(8,128)(2,1)} %param.10, f32[40,32]{1,0:T(8,128)S(1)} %get-tuple-element.4, f32[40,32,128]{2,1,0:T(8,128)S(1)} %get-tuple-element.6, f32[40,32]{1,0:T(8,128)S(1)} %get-tuple-element.5, pred[40,128]{1,0:T(8,128)(4,1)S(1)} %broadcast_compare_fusion.1), kind=kOutput, calls=%fused_computation.3 | convolution fusion | flops 168919040 | bytes 8535040 | tf_op jit(solution)/shard_map/shc,scl->shl/dot_general | solution.py:72
  118.3 3.0 copy.51
  121.4 0.6 copy-done.3
  122.6 24.0 %all-gather = bf16[16,448,40]{1,2,0:T(8,128)(2,1)S(1)} all-gather(bf16[1,448,40]{1,2,0:T(8,128)(2,1)S(1)} %bitcast.43), channel_id=1, replica_groups=mesh['groups'=2,'kv'=16] {'kv'}, dimensions={0}, use_global_device_ids=true | all-gather | bytes 609280 | tf_op jit(solution)/shard_map/all_gather | solution.py:111
  146.6 55.1 %psum.14 = f32[40,32]{1,0:T(8,128)S(1)} all-reduce(f32[40,32]{1,0:T(8,128)S(1)} %get-tuple-element.3), channel_id=1, replica_groups=mesh['groups'=2,'kv'=16] {'kv'}, use_global_device_ids=true, to_apply=%region_6.7 | all-reduce | flops 1280 | bytes 10240 | tf_op jit(solution)/shard_map/psum | solution.py:85
  201.7 1.1 reshape.113
  203.2 3.8 %fusion.17 = f32[40,7168]{1,0:T(8,128)} fusion(bf16[256,7168]{1,0:T(8,128)(2,1)} %param.13, bf16[2,5,8,128]{3,2,1,0:T(8,128)(2,1)S(1)} %fusion.6), kind=kOutput, calls=%fused_computation.28 | convolution fusion | flops 146800640 | bytes 4837376 | tf_op jit(solution)/shard_map/dot_general | solution.py:102
  207.3 0.5 reshape.125
  207.9 0.6 dynamic-slice
  209.4 57.8 %all-reduce = bf16[7168]{0:T(1024)(128)(2,1)S(1)} all-reduce(bf16[7168]{0:T(1024)(128)(2,1)S(1)} %dynamic-update-slice), channel_id=1, replica_groups=mesh['groups'=2,'kv'=16] {'kv'}, use_global_device_ids=true, to_apply=%add | all-reduce | flops 7168 | bytes 28672
  267.7 0.8 fusion.15
  268.5 33.6 %all-reduce.3.cloned.1.call-done = f32[40,7168]{1,0:T(8,128)} async-done(((f32[40,7168]{1,0:T(8,128)}), f32[40,7168]{1,0:T(8,128)}) %all-reduce.3.cloned.1.call-update) | async-done | bytes 1146896 | tf_op jit(solution)/shard_map/psum | solution.py:109
  302.1 1.6 multiply_reduce_fusion
  303.7 0.4 abs_reduce_fusion
  304.1 0.4 convolution_convert_fusion
  304.5 0.9 reshape.116
  305.4 0.8 fusion.20
  (43 shorter events, 2.2 us)
Async XLA Ops:
  7.2 195.8 %copy-start = (bf16[1024,128]{1,0:T(8,128)(2,1)S(1)}, bf16[1024,128]{1,0:T(8,128)(2,1)}, u32[]{:S(2)}) copy-start(bf16[1024,128]{1,0:T(8,128)(2,1)} %param.12) | copy-start | bytes 786436
  7.2 44.8 %all-gather.3.cloned.1.call-start = ((), (), s32[]{:S(2)}) async-start(), calls=%async_computation.1 | async-start | bytes 1566720 | tf_op jit(solution)/shard_map/all_gather | solution.py:60
  7.9 193.8 %reduce-scatter.2.cloned.1.call-start = ((), (), s32[]{:S(2)}) async-start(), calls=%async_computation.2 | async-start | bytes 2785280 | tf_op jit(solution)/shard_map/reduce_scatter | solution.py:87
  121.3 0.7 copy-start.3
  121.3 1.3 copy-start.2
  121.3 180.7 %all-reduce.3.cloned.1.call-start = ((), (), s32[]{:S(2)}) async-start(), calls=%async_computation.3 | async-start | bytes 2293760 | tf_op jit(solution)/shard_map/psum | solution.py:109
  207.3 0.7 copy-start.6
  207.3 1.9 copy-start.5
  207.3 60.0 %copy-start.4 = (f32[40,8]{0,1:T(8,128)S(1)}, f32[40,8]{0,1:T(8,128)}, u32[]{:S(2)}) copy-start(f32[40,8]{0,1:T(8,128)} %param.17) | copy-start | bytes 3844
  302.1 1.6 copy-start.1
Sparse Core Ops, SparseCore 0:
  10.2 41.7 all-gather.2
  121.4 64.1 reduce-scatter.1
  207.2 94.8 all-reduce.2
where the time goes:
time: 315 us; the launch traced here: 313 us
  blocking collectives  192 us (61%)
  waiting for transfers between devices  77.6 us (25%)
  between operations  14.6 us (5%)
  matrix products  13.9 us (4%)
  local copies, waits for them, and re-layouts  11.1 us (4%)
  other arithmetic  3.73 us (1%)
    unnamed x1, blocking collectives  57.8 us
    psum x1, blocking collectives, per_device(): weight_total = lax.psum(local_total * scaling, 'kv')  55.1 us
    pmax x1, blocking collectives, per_device(): global_max = lax.pmax(local_max, 'kv')  54.8 us
    all_gather x1, waiting for transfers between devices, per_device(): lax.all_gather(queries, 'kv', axis=1, tiled=True)  43.3 us
    psum x1, waiting for transfers between devices, per_device(): attn_rows = lax.psum(partial_out, 'kv')  33.6 us
    all_gather x1, blocking collectives, per_device(): lax.all_gather(residual, 'kv', axis=1, tiled=True)  24 us
  transfers between devices with their start and end apart: 3, of which 2 were waited for; matrix products, arithmetic and copies ran while one was open for 1% of the time, Pallas kernels for 0%

commit v1 on v0

--- a/solution.py
+++ b/solution.py
@@ -1,6 +1,10 @@
+import functools
+
 import jax
 import jax.numpy as jnp
 from jax import lax
+from jax.experimental import pallas as pl
+from jax.experimental.pallas import tpu as pltpu
 from jax.sharding import PartitionSpec as P
 
 H = 32
@@ -43,7 +47,7 @@
     return jnp.sum(matches.reshape(matches.shape[0], seq_count, TOPK), axis=2)
 
 
-def per_device(
+def general_device(
     queries,
     latent_cache,
     context_lengths,
@@ -127,6 +131,518 @@
     )
 
 
+CORES = 2
+LINKED_Y = 2
+LANES = 128
+ROWS = 8
+F32 = jnp.float32
+BF16 = jnp.bfloat16
+
+
+def split3(value):
+    first = value.astype(BF16).astype(F32)
+    rest = value - first
+    second = rest.astype(BF16).astype(F32)
+    return first, second, rest - second
+
+
+def put_lanes(shape, columns):
+    lane = lax.broadcasted_iota(jnp.int32, shape, len(shape) - 1)
+    tile = jnp.zeros(shape, F32)
+    for index, column in columns:
+        tile = jnp.where(lane == index, column, tile)
+    return tile
+
+
+def take3(tile, start):
+    return (
+        tile[..., start : start + 1]
+        + tile[..., start + 1 : start + 2]
+        + tile[..., start + 2 : start + 3]
+    )
+
+
+def merge(blocks):
+    heads = (blocks[0].shape[-1] - LANES) // LAT
+    outs, columns = [], []
+    for head in range(heads):
+        stats = [block[..., heads * LAT :] for block in blocks]
+        maxes = [take3(stat, head * 6) for stat in stats]
+        totals = [take3(stat, head * 6 + 3) for stat in stats]
+        top = maxes[0]
+        for other in maxes[1:]:
+            top = jnp.maximum(top, other)
+        total, out = 0.0, 0.0
+        for block, own_max, own_total in zip(blocks, maxes, totals):
+            factor = jnp.exp(own_max - top)
+            total = total + factor * own_total
+            out = out + factor * block[..., head * LAT : (head + 1) * LAT]
+        outs.append((out, top, total))
+    return outs
+
+
+def message(outs):
+    columns = []
+    for head, (out, top, total) in enumerate(outs):
+        for index, part in enumerate(split3(top) + split3(total)):
+            columns.append((head * 6 + index, part))
+    shape = outs[0][0].shape[:-1] + (LANES,)
+    return jnp.concatenate([out for out, _, _ in outs] + [put_lanes(shape, columns)], axis=-1)
+
+
+def step_kernel(
+    zs,
+    chunks,
+    q_ref,
+    cache_hbm,
+    ctx_ref,
+    up_ref,
+    proj_hbm,
+    resid_ref,
+    gain_ref,
+    pick_ref,
+    out_ref,
+    scale_ref,
+    cache,
+    proj,
+    qbuf,
+    qrow,
+    osc,
+    msc,
+    s1,
+    r1,
+    k1,
+    r2,
+    k2,
+    r3,
+    merged,
+    part,
+    ps1,
+    pr1,
+    pk1,
+    pr2,
+    pk2,
+    pr3,
+    gbuf,
+    gainbuf,
+    load_sem,
+    proj_sem,
+    qz_s,
+    qz_r,
+    q_s,
+    q_r,
+    oz_s,
+    oz_r,
+    o_s,
+    o_r,
+    pz_s,
+    pz_r,
+    p_s,
+    p_r,
+):
+    me = lax.axis_index("kv")
+    core = lax.rem(me, CORES)
+    y = lax.rem(me // CORES, LINKED_Y)
+    z = me // (CORES * LINKED_Y)
+
+    def device(zz, yy, cc):
+        return {"kv": (zz * LINKED_Y + yy) * CORES + cc}
+
+    partner = device(z, y, 1 - core)
+    across = device(z, 1 - y, core)
+    along = [lax.rem(z + step, zs) for step in range(1, zs)]
+    back = [lax.rem(z + zs - step, zs) for step in range(1, zs)]
+
+    def copy(source, target, send, recv, where):
+        return pltpu.make_async_remote_copy(
+            src_ref=source,
+            dst_ref=target,
+            send_sem=send,
+            recv_sem=recv,
+            device_id=where,
+            device_id_type=pl.DeviceIdType.MESH,
+        )
+
+    loads = [
+        pltpu.make_async_copy(
+            cache_hbm.at[pl.ds(k * ROWS, ROWS)], cache.at[pl.ds(k * ROWS, ROWS)], load_sem.at[k]
+        )
+        for k in range(chunks)
+    ]
+    for load in loads:
+        load.start()
+    proj_load = pltpu.make_async_copy(proj_hbm, proj, proj_sem)
+    proj_load.start()
+
+    barrier = pltpu.get_barrier_semaphore()
+    peers = [partner, across] + [device(zz, y, core) for zz in along]
+    for peer in peers:
+        pl.semaphore_signal(
+            barrier, inc=1, device_id=peer, device_id_type=pl.DeviceIdType.MESH
+        )
+    pl.semaphore_wait(barrier, len(peers))
+
+    pending = []
+
+    def z_copies(source_of, target, send, recv):
+        made = []
+        for step, zz in enumerate(along):
+            made.append(copy(source_of(zz), target, send.at[step], recv.at[step], device(zz, y, core)))
+        return made
+
+    def launch(made):
+        for one in made:
+            one.start()
+            pending.append(one)
+        return made
+
+    gain_copy = launch(
+        [copy(gain_ref, gainbuf, p_s.at[4], p_r.at[4], partner)]
+    )
+    q_along = [
+        launch(z_copies(lambda zz: q_ref.at[k], qbuf.at[k, core, y, z], qz_s.at[k], qz_r.at[k]))
+        for k in range(chunks)
+    ]
+    for k in range(chunks):
+        qbuf[k, core, y, z] = q_ref[k]
+    q_across, q_pair, o_pair, o_across, o_along = {}, {}, {}, {}, {}
+
+    def gather_across(k):
+        for one in q_along[k]:
+            one.wait_recv()
+        q_across[k] = launch(
+            [copy(qbuf.at[k, core, y], qbuf.at[k, core, y], q_s.at[k, 0], q_r.at[k, 0], across)]
+        )
+
+    def gather_pair(k):
+        q_across[k][0].wait_recv()
+        q_pair[k] = launch(
+            [copy(qbuf.at[k, core], qbuf.at[k, core], q_s.at[k, 1], q_r.at[k, 1], partner)]
+        )
+
+    ctx_local = cache.shape[1]
+    count = CORES * LINKED_Y * zs
+    position = me * ctx_local + lax.broadcasted_iota(jnp.int32, (2 * count, ctx_local), 1)
+
+    def attend(k):
+        q_pair[k][0].wait_recv()
+        loads[k].wait()
+        width = q_ref.shape[-1]
+        rows = qbuf[k].reshape(count, ROWS, width).astype(F32)
+        qrow[...] = jnp.swapaxes(rows, 0, 1).astype(BF16)
+
+        def one(s, carry):
+            row = qrow[s]
+            keys = cache[k * ROWS + s]
+            latent = jnp.concatenate([row[:, :LAT], row[:, LAT : 2 * LAT]], axis=0)
+            rotary = row[:, 2 * LAT :]
+            rotary = jnp.concatenate([rotary[:, :ROPE], rotary[:, ROPE:]], axis=0)
+            over = (((1,), (1,)), ((), ()))
+            scores = lax.dot_general(latent, keys[:, :LAT], over, preferred_element_type=F32)
+            scores = scores + lax.dot_general(
+                rotary, keys[:, LAT:], over, preferred_element_type=F32
+            )
+            valid = position < ctx_ref[k * ROWS + s]
+            scores = jnp.where(valid, scores * score_scale, masked_score)
+            top = jnp.max(scores, axis=1, keepdims=True)
+            weights = jnp.where(valid, jnp.exp(scores - top), 0.0)
+            total = jnp.sum(weights, axis=1, keepdims=True)
+            osc[s] = jnp.dot(weights.astype(BF16), keys[:, :LAT], preferred_element_type=F32)
+            columns = []
+            for head in range(2):
+                here = slice(head * count, (head + 1) * count)
+                parts = split3(top[here]) + split3(total[here])
+                columns += [(head * 6 + index, value) for index, value in enumerate(parts)]
+            msc[s] = put_lanes((count, LANES), columns)
+            return carry
+
+        lax.fori_loop(0, ROWS, one, 0)
+        whole = jnp.swapaxes(osc[...], 0, 1).astype(BF16)
+        shape = (CORES, LINKED_Y, zs, ROWS)
+        s1[k, :, :, :, :, :LAT] = whole[:count].reshape(shape + (LAT,))
+        s1[k, :, :, :, :, LAT : 2 * LAT] = whole[count:].reshape(shape + (LAT,))
+        s1[k, :, :, :, :, 2 * LAT :] = (
+            jnp.swapaxes(msc[...], 0, 1).astype(BF16).reshape(shape + (LANES,))
+        )
+        o_pair[k] = launch([copy(s1.at[k, 1 - core], r1.at[k], o_s.at[k, 0], o_r.at[k, 0], partner)])
+
+    def merge_pair(k):
+        o_pair[k][0].wait_recv()
+
+        def one(i, carry):
+            k1[k, 1 - y, i] = message(
+                merge([s1[k, core, 1 - y, i].astype(F32), r1[k, 1 - y, i].astype(F32)])
+            ).astype(BF16)
+            return carry
+
+        lax.fori_loop(0, zs, one, 0)
+        o_across[k] = launch([copy(k1.at[k, 1 - y], r2.at[k], o_s.at[k, 1], o_r.at[k, 1], across)])
+
+    def merge_across(k):
+        o_across[k][0].wait_recv()
+
+        def one(i, carry):
+            k2[k, i] = message(
+                merge(
+                    [
+                        s1[k, core, y, i].astype(F32),
+                        r1[k, y, i].astype(F32),
+                        r2[k, i].astype(F32),
+                    ]
+                )
+            ).astype(BF16)
+            return carry
+
+        lax.fori_loop(0, zs, one, 0)
+        o_along[k] = launch(
+            [
+                copy(k2.at[k, zz], r3.at[k, step], oz_s.at[k, step], oz_r.at[k, step], device(zz, y, core))
+                for step, zz in enumerate(along)
+            ]
+        )
+
+    def merge_along(k):
+        for one in o_along[k]:
+            one.wait_recv()
+        blocks = [k2[k, z].astype(F32)] + [r3[k, step].astype(F32) for step in range(zs - 1)]
+        for head, (out, _, total) in enumerate(merge(blocks)):
+            merged[head, pl.ds(k * ROWS, ROWS), :] = out / total
+
+    for t in range(chunks + 5):
+        for stage, lag in (
+            (gather_across, 0),
+            (gather_pair, 1),
+            (attend, 2),
+            (merge_pair, 3),
+            (merge_across, 4),
+            (merge_along, 5),
+        ):
+            if 0 <= t - lag < chunks:
+                stage(t - lag)
+
+    values = []
+    for head in range(2):
+        own = merged[head]
+        high = own.astype(BF16)
+        low = (own - high.astype(F32)).astype(BF16)
+        rows = up_ref[head * LAT : (head + 1) * LAT]
+        values.append(
+            jnp.dot(high, rows, preferred_element_type=F32)
+            + jnp.dot(low, rows, preferred_element_type=F32)
+        )
+    value = jnp.concatenate(values, axis=1).astype(BF16)
+    proj_load.wait()
+    chip_cols = part.shape[-1]
+    held = ps1.shape[-1]
+    skip = chip_cols - held
+    for zz in range(zs):
+        for yy in range(LINKED_Y):
+            start = (zz * LINKED_Y + yy) * chip_cols
+            part[yy, zz] = jnp.dot(
+                value, proj[:, start : start + chip_cols], preferred_element_type=F32
+            )
+    part[y, z] = part[y, z] + resid_ref[...].astype(F32)
+    own_cols = pl.ds(pl.multiple_of(core * skip, LANES), held)
+    other_cols = pl.ds(pl.multiple_of((1 - core) * skip, LANES), held)
+    ps1[...] = part[:, :, :, other_cols].astype(BF16)
+    p_pair = launch([copy(ps1, pr1, p_s.at[0], p_r.at[0], partner)])
+    p_pair[0].wait_recv()
+    pk1[...] = (part[1 - y, :, :, own_cols] + pr1[1 - y].astype(F32)).astype(BF16)
+    p_across = launch([copy(pk1, pr2, p_s.at[1], p_r.at[1], across)])
+    p_across[0].wait_recv()
+    kept = part[y, :, :, own_cols] + pr1[y].astype(F32) + pr2[...].astype(F32)
+    part[y, :, :, own_cols] = kept
+    pk2[...] = kept.astype(BF16)
+    p_along = launch(
+        [
+            copy(pk2.at[zz], pr3.at[step], pz_s.at[0, step], pz_r.at[0, step], device(zz, y, core))
+            for step, zz in enumerate(along)
+        ]
+    )
+    gain_copy[0].wait_recv()
+    for one in p_along:
+        one.wait_recv()
+    summed = part[y, z, :, own_cols]
+    for step in range(zs - 1):
+        summed = summed + pr3[step].astype(F32)
+    gain = (gain_ref[...].astype(F32) + gainbuf[...].astype(F32))[:1]
+    gain = jnp.where(core == 0, gain[:, :held], gain[:, skip:])
+    scaled = summed * gain
+    lane = lax.broadcasted_iota(jnp.int32, summed.shape, 1)
+    first = jnp.where(core == 0, 0, 2 * held - chip_cols)
+    square = jnp.sum(jnp.where(lane >= first, summed * summed, 0.0), axis=1, keepdims=True)
+    largest = jnp.max(jnp.abs(scaled), axis=1, keepdims=True)
+    columns = list(enumerate(split3(square) + split3(largest)))
+    stats = put_lanes((summed.shape[0], LANES), columns)
+    gbuf[core, y, z] = jnp.concatenate([scaled, stats], axis=1).astype(BF16)
+    g_along = launch(
+        [
+            copy(
+                gbuf.at[core, y, z],
+                gbuf.at[core, y, z],
+                pz_s.at[1, step],
+                pz_r.at[1, step],
+                device(zz, y, core),
+            )
+            for step, zz in enumerate(along)
+        ]
+    )
+    for one in g_along:
+        one.wait_recv()
+    g_across = launch([copy(gbuf.at[core, y], gbuf.at[core, y], p_s.at[2], p_r.at[2], across)])
+    g_across[0].wait_recv()
+    g_pair = launch([copy(gbuf.at[core], gbuf.at[core], p_s.at[3], p_r.at[3], partner)])
+    g_pair[0].wait_recv()
+
+    stats = gbuf[:, :, :, :, held:].astype(F32).reshape(count, summed.shape[0], LANES)
+    square = jnp.sum(take3(stats, 0), axis=0)
+    largest = jnp.max(take3(stats, 3), axis=0)
+    inverse = lax.rsqrt(square / (chip_cols * LINKED_Y * zs) + small_eps)
+    peak = largest * inverse + small_eps
+    factor = inverse / peak
+    pick = pick_ref[...].astype(BF16)
+    for zz in range(zs):
+        for yy in range(LINKED_Y):
+            start = (zz * LINKED_Y + yy) * chip_cols
+            for cc in range(CORES):
+                drop = cc * (2 * held - chip_cols)
+                rows = gbuf[cc, yy, zz, :, drop:held].astype(F32) * factor
+                at = start + cc * held
+                out_ref[:, at : at + held - drop] = jnp.dot(
+                    pick, rows.astype(BF16), preferred_element_type=F32
+                ).astype(BF16)
+    scale_ref[...] = jnp.dot(
+        pick_ref[...],
+        jnp.broadcast_to(peak, (peak.shape[0], LANES)),
+        precision=lax.Precision.HIGHEST,
+        preferred_element_type=F32,
+    )
+    for one in pending:
+        one.wait_send()
+
+
+def fused_device(
+    queries,
+    latent_cache,
+    context_lengths,
+    value_up,
+    out_proj,
+    residual,
+    norm_gain,
+    expert_ids,
+    gate_weights,
+):
+    kv_count = lax.axis_size("kv")
+    shard_index = lax.axis_index("kv")
+    core = shard_index % CORES
+    zs = kv_count // (CORES * LINKED_Y)
+    seq_count = queries.shape[0]
+    chunks = seq_count // ROWS
+    ctx_local = latent_cache.shape[1]
+    width = queries.shape[1]
+    cols = residual.shape[1]
+    chip_cols = cols * CORES
+    held = -(-cols // LANES) * LANES
+    heads = queries.reshape(seq_count, H // kv_count, LAT + ROPE)
+    rows = jnp.concatenate(
+        [heads[:, :, :LAT].reshape(seq_count, -1), heads[:, :, LAT:].reshape(seq_count, -1)], axis=1
+    ).reshape(chunks, ROWS, width)
+
+    def placed(block):
+        zero = jnp.zeros_like(block)
+        return jnp.concatenate(
+            [jnp.where(core == 0, block, zero), jnp.where(core == 0, zero, block)], axis=1
+        )
+
+    gain = placed(jnp.broadcast_to(norm_gain[None, :], (ROWS, cols)))
+    experts_local = EXPERTS // kv_count
+    slot_count = experts_local * CAP
+    targets = slot_targets(expert_ids)
+    own_match = slot_match(targets, shard_index * slot_count, slot_count)
+    own_pick = token_picker(own_match, seq_count)
+    slot_gate = jnp.sum(own_match * gate_weights.reshape(1, -1), axis=1)
+
+    vmem = pl.BlockSpec(memory_space=pltpu.VMEM)
+    smem = pl.BlockSpec(memory_space=pltpu.SMEM)
+    anywhere = pl.BlockSpec(memory_space=pl.ANY)
+    dma = pltpu.SemaphoreType.DMA
+    full = (LINKED_Y, zs)
+    dispatched, scale = pl.pallas_call(
+        functools.partial(step_kernel, zs, chunks),
+        out_shape=(
+            jax.ShapeDtypeStruct((slot_count, chip_cols * LINKED_Y * zs), BF16),
+            jax.ShapeDtypeStruct((slot_count, LANES), F32),
+        ),
+        in_specs=[vmem, anywhere, smem, vmem, anywhere, vmem, vmem, vmem],
+        out_specs=(vmem, vmem),
+        scratch_shapes=[
+            pltpu.VMEM(latent_cache.shape, BF16),
+            pltpu.VMEM(out_proj.shape, BF16),
+            pltpu.VMEM((chunks, CORES) + full + (ROWS, width), BF16),
+            pltpu.VMEM((ROWS, kv_count, width), BF16),
+            pltpu.VMEM((ROWS, H, LAT), F32),
+            pltpu.VMEM((ROWS, kv_count, LANES), F32),
+            pltpu.VMEM((chunks, CORES) + full + (ROWS, width), BF16),
+            pltpu.VMEM((chunks,) + full + (ROWS, width), BF16),
+            pltpu.VMEM((chunks,) + full + (ROWS, width), BF16),
+            pltpu.VMEM((chunks, zs, ROWS, width), BF16),
+            pltpu.VMEM((chunks, zs, ROWS, width), BF16),
+            pltpu.VMEM((chunks, zs - 1, ROWS, width), BF16),
+            pltpu.VMEM((H // kv_count, seq_count, LAT), F32),
+            pltpu.VMEM(full + (seq_count, chip_cols), F32),
+            pltpu.VMEM(full + (seq_count, held), BF16),
+            pltpu.VMEM(full + (seq_count, held), BF16),
+            pltpu.VMEM((zs, seq_count, held), BF16),
+            pltpu.VMEM((zs, seq_count, held), BF16),
+            pltpu.VMEM((zs, seq_count, held), BF16),
+            pltpu.VMEM((zs - 1, seq_count, held), BF16),
+            pltpu.VMEM((CORES,) + full + (seq_count, held + LANES), BF16),
+            pltpu.VMEM((ROWS, chip_cols), BF16),
+            dma((chunks,)),
+            dma,
+            dma((chunks, zs - 1)),
+            dma((chunks, zs - 1)),
+            dma((chunks, 2)),
+            dma((chunks, 2)),
+            dma((chunks, zs - 1)),
+            dma((chunks, zs - 1)),
+            dma((chunks, 2)),
+            dma((chunks, 2)),
+            dma((2, zs - 1)),
+            dma((2, zs - 1)),
+            dma((5,)),
+            dma((5,)),
+        ],
+        compiler_params=pltpu.CompilerParams(
+            collective_id=0, has_side_effects=True, vmem_limit_bytes=60 * 1024 * 1024
+        ),
+    )(
+        rows,
+        latent_cache,
+        context_lengths,
+        value_up,
+        out_proj,
+        placed(residual),
+        gain,
+        own_pick,
+    )
+    return (
+        dispatched.reshape(experts_local, CAP, -1),
+        scale[:, 0].reshape(experts_local, CAP),
+        slot_gate.reshape(experts_local, CAP),
+    )
+
+
+def per_device(*arrays):
+    queries, residual = arrays[0], arrays[5]
+    kv_count = lax.axis_size("kv")
+    pairs = H == 2 * kv_count and 2 * ROPE == LANES and kv_count % (CORES * LINKED_Y) == 0
+    aligned = queries.shape[0] % ROWS == 0 and residual.shape[1] * CORES % LANES == 0
+    if pairs and aligned:
+        return fused_device(*arrays)
+    return general_device(*arrays)
+
+
 def solution(mesh):
     in_specs = (
         P("groups", "kv"),

time: 315 us -> 101 us (0.32)
  blocking collectives: 192 us -> 0 us
  Pallas kernels: 0 us -> 78.5 us
  waiting for transfers between devices: 77.6 us -> 0 us
  matrix products: 13.9 us -> 0 us
  between operations: 14.6 us -> 0.71 us
  local copies, waits for them, and re-layouts: 11.1 us -> 16.5 us
    pallas_call x0 -> x1, Pallas kernels: none -> 78.5 us  [fused_device(): pl.pallas_call(functools.partial(step_kernel, zs, chunks), out_shape=(jax...]
    unnamed x1 -> x0, blocking collectives: 57.8 us -> none
    psum x1 -> x0, blocking collectives: 55.1 us -> none  [per_device(): weight_total = lax.psum(local_total * scaling, 'kv')]
    pmax x1 -> x0, blocking collectives: 54.8 us -> none  [per_device(): global_max = lax.pmax(local_max, 'kv')]
    all_gather x1 -> x0, waiting for transfers between devices: 43.3 us -> none  [per_device(): lax.all_gather(queries, 'kv', axis=1, tiled=True)]
    psum x1 -> x0, waiting for transfers between devices: 33.6 us -> none  [per_device(): attn_rows = lax.psum(partial_out, 'kv')]
    all_gather x1 -> x0, blocking collectives: 24 us -> none  [per_device(): lax.all_gather(residual, 'kv', axis=1, tiled=True)]
    dot_general x7 -> x0, matrix products: 13.9 us -> none  [the longest x1 3.9 us: per_device(): jnp.einsum('shc,scl->shl', weights.astype(jnp.bfloat16), latent_cache[:,...]
  transfers between devices with their start and end apart: 3 -> 0, of which waited for: 2 -> 0; matrix products, arithmetic and copies ran while one was open for 1% -> 0% of each run, Pallas kernels for 0% -> 0%
where the time goes in v1:
time: 101 us
  Pallas kernels  78.5 us (78%)
  local copies, waits for them, and re-layouts  16.5 us (16%)
  other arithmetic  4.75 us (5%)
    pallas_call x1, Pallas kernels, fused_device(): pl.pallas_call(functools.partial(step_kernel, zs, chunks), out_shape=(jax...  78.5 us
    unnamed x5, local copies, waits for them, and re-layouts  11.4 us

profile of v1, /device:TPU:1, one launch (start us, length us, event | category | flops | bytes accessed | tf_op | source)
XLA Modules:
  0.0 100.5 jit_solution(9347322090557423684)
XLA Ops:
  0.7 0.7 broadcast_select_fusion.3
  1.4 0.6 broadcast.29.gain_ref
  2.0 0.8 copy.32
  2.8 0.1 mul.33
  2.9 0.8 copy.29
  3.6 0.1 eq.45
  3.7 0.2 convert_reduce_fusion
  4.0 0.2 select_reduce_fusion
  4.1 0.1 reshape.54
  4.2 0.7 copy.34
  4.9 0.1 reduce_sum.30
  5.0 0.7 multiply_add_fusion
  5.7 0.7 convert_reduce_fusion.1.pick_ref
  6.5 0.8 broadcast_select_fusion.1
  7.2 0.7 pad_maximum_fusion.1.resid_ref
  8.0 1.0 %reshape.52 = bf16[40,2,576]{2,1,0:T(2,128)(2,1)S(1)} reshape(bf16[40,1152]{1,0:T(8,128)(2,1)} %param.9) | data formatting | bytes 184320 | tf_op jit(solution)/shard_map/reshape | solution.py:546
  9.1 0.1 concatenate.15
  9.2 0.6 pad_maximum_fusion.q_ref
  9.9 8.6 %copy.31.cache_hbm = bf16[40,128,576]{2,1,0:T(8,128)(2,1)} copy(bf16[40,128,576]{1,2,0:T(8,128)(2,1)} %param.10) | data formatting | bytes 11796480 | tf_op args[1]
  18.5 78.5 %shard_map.112 = (bf16[32,7168]{1,0:T(8,128)(2,1)}, f32[32,128]{1,0:T(8,128)}) custom-call(bf16[5,8,1152]{2,1,0:T(8,128)(2,1)} %pad_maximum_fusion.q_ref, bf16[40,128,576]{2,1,0:T(8,128)(2,1)} %copy.31.cache_hbm, s32[40]{0:T(128)} %ctx_ref.1, bf16[1024,128]{1,0:T(8,128)(2,1)} %up_ref.1, bf16[256,7168]{1,0:T(8,128)(2,1)} %proj_hbm.1, ...), custom_call_target="tpu_custom_call" | custom-call | tf_op jit(solution)/shard_map/pallas_call | solution.py:570
  97.0 2.0 %reshape.53 = bf16[16,2,7168]{2,1,0:T(2,128)(2,1)} reshape(bf16[32,7168]{1,0:T(8,128)(2,1)} %get-tuple-element.5) | data formatting | bytes 917504 | tf_op jit(solution)/shard_map/reshape | solution.py:630
  98.9 0.8 slice_reduce_fusion
  99.8 0.1 reshape_squeeze.3
  99.9 0.7 copy.33
  (7 shorter events, 0.3 us)

commit v2 on v1

--- a/solution.py
+++ b/solution.py
@@ -200,9 +200,13 @@
     proj_hbm,
     resid_ref,
     gain_ref,
-    pick_ref,
+    ids_ref,
+    gates_ref,
     out_ref,
     scale_ref,
+    qown,
+    gainown,
+    pick_scr,
     cache,
     proj,
     qbuf,
@@ -274,6 +278,44 @@
     proj_load = pltpu.make_async_copy(proj_hbm, proj, proj_sem)
     proj_load.start()
 
+    raw = q_ref[...].astype(F32)
+    key = LAT + ROPE
+    qown[...] = jnp.concatenate(
+        [raw[..., :LAT], raw[..., key : key + LAT], raw[..., LAT:key], raw[..., key + LAT :]],
+        axis=-1,
+    ).astype(BF16)
+
+    def placed(block):
+        zero = jnp.zeros_like(block)
+        return jnp.where(
+            core == 0,
+            jnp.concatenate([block, zero], axis=-1),
+            jnp.concatenate([zero, block], axis=-1),
+        )
+
+    gainown[...] = placed(
+        jnp.broadcast_to(gain_ref[...].astype(F32), (ROWS, gain_ref.shape[-1]))
+    ).astype(BF16)
+
+    ids, gates = ids_ref[...], gates_ref[...]
+    slots, seqs = out_ref.shape[0], ids.shape[1]
+    experts = slots // CAP
+    expert = me * experts + lax.broadcasted_iota(jnp.int32, (experts, seqs), 0)
+    member, gate = jnp.zeros((experts, seqs), F32), jnp.zeros((experts, seqs), F32)
+    for choice in range(ids.shape[0]):
+        same = ids[choice : choice + 1] == expert
+        member = jnp.where(same, 1.0, member)
+        gate = jnp.where(same, gates[choice : choice + 1], gate)
+    earlier = lax.broadcasted_iota(jnp.int32, (seqs, seqs), 0) < lax.broadcasted_iota(
+        jnp.int32, (seqs, seqs), 1
+    )
+    rank = jnp.dot(
+        member.astype(BF16), earlier.astype(F32).astype(BF16), preferred_element_type=F32
+    )
+    picks = [jnp.where(jnp.abs(rank - slot) < 0.5, member, 0.0) for slot in range(CAP)]
+    pick_scr[...] = jnp.concatenate(picks, axis=0)
+    slot_gates = [jnp.sum(pick * gate, axis=1, keepdims=True) for pick in picks]
+
     barrier = pltpu.get_barrier_semaphore()
     peers = [partner, across] + [device(zz, y, core) for zz in along]
     for peer in peers:
@@ -297,14 +339,14 @@
         return made
 
     gain_copy = launch(
-        [copy(gain_ref, gainbuf, p_s.at[4], p_r.at[4], partner)]
+        [copy(gainown, gainbuf, p_s.at[4], p_r.at[4], partner)]
     )
     q_along = [
-        launch(z_copies(lambda zz: q_ref.at[k], qbuf.at[k, core, y, z], qz_s.at[k], qz_r.at[k]))
+        launch(z_copies(lambda zz: qown.at[k], qbuf.at[k, core, y, z], qz_s.at[k], qz_r.at[k]))
         for k in range(chunks)
     ]
     for k in range(chunks):
-        qbuf[k, core, y, z] = q_ref[k]
+        qbuf[k, core, y, z] = qown[k]
     q_across, q_pair, o_pair, o_across, o_along = {}, {}, {}, {}, {}
 
     def gather_across(k):
@@ -320,7 +362,7 @@
             [copy(qbuf.at[k, core], qbuf.at[k, core], q_s.at[k, 1], q_r.at[k, 1], partner)]
         )
 
-    ctx_local = cache.shape[1]
+    ctx_local = cache.shape[2]
     count = CORES * LINKED_Y * zs
     position = me * ctx_local + lax.broadcasted_iota(jnp.int32, (2 * count, ctx_local), 1)
 
@@ -331,32 +373,36 @@
         rows = qbuf[k].reshape(count, ROWS, width).astype(F32)
         qrow[...] = jnp.swapaxes(rows, 0, 1).astype(BF16)
 
-        def one(s, carry):
-            row = qrow[s]
-            keys = cache[k * ROWS + s]
+        scored = []
+        for at in range(ROWS):
+            row = qrow[at]
             latent = jnp.concatenate([row[:, :LAT], row[:, LAT : 2 * LAT]], axis=0)
             rotary = row[:, 2 * LAT :]
             rotary = jnp.concatenate([rotary[:, :ROPE], rotary[:, ROPE:]], axis=0)
-            over = (((1,), (1,)), ((), ()))
-            scores = lax.dot_general(latent, keys[:, :LAT], over, preferred_element_type=F32)
-            scores = scores + lax.dot_general(
-                rotary, keys[:, LAT:], over, preferred_element_type=F32
+            scores = jnp.dot(latent, cache[k * ROWS + at, :LAT], preferred_element_type=F32)
+            scores = scores + jnp.dot(
+                rotary, cache[k * ROWS + at, LAT:], preferred_element_type=F32
             )
-            valid = position < ctx_ref[k * ROWS + s]
-            scores = jnp.where(valid, scores * score_scale, masked_score)
-            top = jnp.max(scores, axis=1, keepdims=True)
-            weights = jnp.where(valid, jnp.exp(scores - top), 0.0)
-            total = jnp.sum(weights, axis=1, keepdims=True)
-            osc[s] = jnp.dot(weights.astype(BF16), keys[:, :LAT], preferred_element_type=F32)
-            columns = []
-            for head in range(2):
-                here = slice(head * count, (head + 1) * count)
-                parts = split3(top[here]) + split3(total[here])
-                columns += [(head * 6 + index, value) for index, value in enumerate(parts)]
-            msc[s] = put_lanes((count, LANES), columns)
-            return carry
-
-        lax.fori_loop(0, ROWS, one, 0)
+            valid = position < ctx_ref[k * ROWS + at]
+            scored.append(jnp.where(valid, scores * score_scale, masked_score))
+        scores = jnp.stack(scored)
+        top = jnp.max(scores, axis=2, keepdims=True)
+        weights = jnp.where(scores > 0.5 * masked_score, jnp.exp(scores - top), 0.0)
+        total = jnp.sum(weights, axis=2, keepdims=True)
+        rounded = weights.astype(BF16)
+        for at in range(ROWS):
+            osc[at] = lax.dot_general(
+                rounded[at],
+                cache[k * ROWS + at, :LAT],
+                (((1,), (1,)), ((), ())),
+                preferred_element_type=F32,
+            )
+        columns = []
+        for head in range(2):
+            here = slice(head * count, (head + 1) * count)
+            parts = split3(top[:, here]) + split3(total[:, here])
+            columns += [(head * 6 + index, value) for index, value in enumerate(parts)]
+        msc[...] = put_lanes((ROWS, count, LANES), columns)
         whole = jnp.swapaxes(osc[...], 0, 1).astype(BF16)
         shape = (CORES, LINKED_Y, zs, ROWS)
         s1[k, :, :, :, :, :LAT] = whole[:count].reshape(shape + (LAT,))
@@ -369,31 +415,17 @@
     def merge_pair(k):
         o_pair[k][0].wait_recv()
 
-        def one(i, carry):
-            k1[k, 1 - y, i] = message(
-                merge([s1[k, core, 1 - y, i].astype(F32), r1[k, 1 - y, i].astype(F32)])
-            ).astype(BF16)
-            return carry
-
-        lax.fori_loop(0, zs, one, 0)
+        k1[k, 1 - y] = message(
+            merge([s1[k, core, 1 - y].astype(F32), r1[k, 1 - y].astype(F32)])
+        ).astype(BF16)
         o_across[k] = launch([copy(k1.at[k, 1 - y], r2.at[k], o_s.at[k, 1], o_r.at[k, 1], across)])
 
     def merge_across(k):
         o_across[k][0].wait_recv()
 
-        def one(i, carry):
-            k2[k, i] = message(
-                merge(
-                    [
-                        s1[k, core, y, i].astype(F32),
-                        r1[k, y, i].astype(F32),
-                        r2[k, i].astype(F32),
-                    ]
-                )
-            ).astype(BF16)
-            return carry
-
-        lax.fori_loop(0, zs, one, 0)
+        k2[k] = message(
+            merge([s1[k, core, y].astype(F32), r1[k, y].astype(F32), r2[k].astype(F32)])
+        ).astype(BF16)
         o_along[k] = launch(
             [
                 copy(k2.at[k, zz], r3.at[k, step], oz_s.at[k, step], oz_r.at[k, step], device(zz, y, core))
@@ -441,7 +473,7 @@
             part[yy, zz] = jnp.dot(
                 value, proj[:, start : start + chip_cols], preferred_element_type=F32
             )
-    part[y, z] = part[y, z] + resid_ref[...].astype(F32)
+    part[y, z] = part[y, z] + placed(resid_ref[...].astype(F32))
     own_cols = pl.ds(pl.multiple_of(core * skip, LANES), held)
     other_cols = pl.ds(pl.multiple_of((1 - core) * skip, LANES), held)
     ps1[...] = part[:, :, :, other_cols].astype(BF16)
@@ -465,7 +497,7 @@
     summed = part[y, z, :, own_cols]
     for step in range(zs - 1):
         summed = summed + pr3[step].astype(F32)
-    gain = (gain_ref[...].astype(F32) + gainbuf[...].astype(F32))[:1]
+    gain = (gainown[...].astype(F32) + gainbuf[...].astype(F32))[:1]
     gain = jnp.where(core == 0, gain[:, :held], gain[:, skip:])
     scaled = summed * gain
     lane = lax.broadcasted_iota(jnp.int32, summed.shape, 1)
@@ -500,7 +532,7 @@
     inverse = lax.rsqrt(square / (chip_cols * LINKED_Y * zs) + small_eps)
     peak = largest * inverse + small_eps
     factor = inverse / peak
-    pick = pick_ref[...].astype(BF16)
+    pick = pick_scr[...].astype(BF16)
     for zz in range(zs):
         for yy in range(LINKED_Y):
             start = (zz * LINKED_Y + yy) * chip_cols
@@ -511,12 +543,16 @@
                 out_ref[:, at : at + held - drop] = jnp.dot(
                     pick, rows.astype(BF16), preferred_element_type=F32
                 ).astype(BF16)
-    scale_ref[...] = jnp.dot(
-        pick_ref[...],
+    scales = jnp.dot(
+        pick_scr[...],
         jnp.broadcast_to(peak, (peak.shape[0], LANES)),
         precision=lax.Precision.HIGHEST,
         preferred_element_type=F32,
     )
+    wide = jnp.broadcast_to(jnp.concatenate(slot_gates, axis=0), (slots, LANES))
+    tail = jnp.zeros((LANES - 2 * slots, LANES), F32)
+    flat = jnp.transpose(jnp.concatenate([scales, wide, tail], axis=0))
+    scale_ref[...] = flat[:ROWS]
     for one in pending:
         one.wait_send()
 
@@ -533,8 +569,6 @@
     gate_weights,
 ):
     kv_count = lax.axis_size("kv")
-    shard_index = lax.axis_index("kv")
-    core = shard_index % CORES
     zs = kv_count // (CORES * LINKED_Y)
     seq_count = queries.shape[0]
     chunks = seq_count // ROWS
@@ -543,25 +577,8 @@
     cols = residual.shape[1]
     chip_cols = cols * CORES
     held = -(-cols // LANES) * LANES
-    heads = queries.reshape(seq_count, H // kv_count, LAT + ROPE)
-    rows = jnp.concatenate(
-        [heads[:, :, :LAT].reshape(seq_count, -1), heads[:, :, LAT:].reshape(seq_count, -1)], axis=1
-    ).reshape(chunks, ROWS, width)
-
-    def placed(block):
-        zero = jnp.zeros_like(block)
-        return jnp.concatenate(
-            [jnp.where(core == 0, block, zero), jnp.where(core == 0, zero, block)], axis=1
-        )
-
-    gain = placed(jnp.broadcast_to(norm_gain[None, :], (ROWS, cols)))
     experts_local = EXPERTS // kv_count
     slot_count = experts_local * CAP
-    targets = slot_targets(expert_ids)
-    own_match = slot_match(targets, shard_index * slot_count, slot_count)
-    own_pick = token_picker(own_match, seq_count)
-    slot_gate = jnp.sum(own_match * gate_weights.reshape(1, -1), axis=1)
-
     vmem = pl.BlockSpec(memory_space=pltpu.VMEM)
     smem = pl.BlockSpec(memory_space=pltpu.SMEM)
     anywhere = pl.BlockSpec(memory_space=pl.ANY)
@@ -571,12 +588,15 @@
         functools.partial(step_kernel, zs, chunks),
         out_shape=(
             jax.ShapeDtypeStruct((slot_count, chip_cols * LINKED_Y * zs), BF16),
-            jax.ShapeDtypeStruct((slot_count, LANES), F32),
+            jax.ShapeDtypeStruct((ROWS, LANES), F32),
         ),
-        in_specs=[vmem, anywhere, smem, vmem, anywhere, vmem, vmem, vmem],
+        in_specs=[vmem, anywhere, smem, vmem, anywhere, vmem, vmem, vmem, vmem],
         out_specs=(vmem, vmem),
         scratch_shapes=[
-            pltpu.VMEM(latent_cache.shape, BF16),
+            pltpu.VMEM((chunks, ROWS, width), BF16),
+            pltpu.VMEM((ROWS, chip_cols), BF16),
+            pltpu.VMEM((slot_count, seq_count), F32),
+            pltpu.VMEM((seq_count, LAT + ROPE, ctx_local), BF16),
             pltpu.VMEM(out_proj.shape, BF16),
             pltpu.VMEM((chunks, CORES) + full + (ROWS, width), BF16),
             pltpu.VMEM((ROWS, kv_count, width), BF16),
@@ -617,26 +637,25 @@
             collective_id=0, has_side_effects=True, vmem_limit_bytes=60 * 1024 * 1024
         ),
     )(
-        rows,
-        latent_cache,
+        queries.reshape(chunks, ROWS, width),
+        jnp.swapaxes(latent_cache, 1, 2),
         context_lengths,
         value_up,
         out_proj,
-        placed(residual),
-        gain,
-        own_pick,
-    )
-    return (
-        dispatched.reshape(experts_local, CAP, -1),
-        scale[:, 0].reshape(experts_local, CAP),
-        slot_gate.reshape(experts_local, CAP),
-    )
+        residual,
+        norm_gain.reshape(1, -1),
+        expert_ids.T,
+        gate_weights.T,
+    )
+    split = jnp.swapaxes(dispatched.reshape(CAP, experts_local, -1), 0, 1)
+    scale = scale[0].reshape(-1, CAP, experts_local)
+    return split, scale[0].T, scale[1].T
 
 
 def per_device(*arrays):
     queries, residual = arrays[0], arrays[5]
     kv_count = lax.axis_size("kv")
-    pairs = H == 2 * kv_count and 2 * ROPE == LANES and kv_count % (CORES * LINKED_Y) == 0
+    pairs = H == 2 * kv_count and EXPERTS * CAP * 2 <= kv_count * LANES and 2 * ROPE == LANES and kv_count % (CORES * LINKED_Y) == 0
     aligned = queries.shape[0] % ROWS == 0 and residual.shape[1] * CORES % LANES == 0
     if pairs and aligned:
         return fused_device(*arrays)

time: 101 us -> 72 us (0.71)
  Pallas kernels: 78.5 us -> 65.5 us
  local copies, waits for them, and re-layouts: 16.5 us -> 5.63 us
  other arithmetic: 4.75 us -> 0 us
    pallas_call x1, Pallas kernels: 78.5 us -> 65.5 us  [fused_device(): pl.pallas_call(functools.partial(step_kernel, zs, chunks), out_shape=(jax...]
    unnamed x5 -> x0, local copies, waits for them, and re-layouts: 11.4 us -> none
    select_n x2 -> x0, other arithmetic: 1.47 us -> none  [placed(): jnp.where(core == 0, block, zero)]
    concatenate x3 -> x0, other arithmetic: 1.44 us -> none  [the longest x2 0.8 us: placed(): jnp.concatenate([jnp.where(core == 0, block, zero), jnp.where(core == 0,...]
    squeeze x0 -> x2, local copies, waits for them, and re-layouts: none -> 1.28 us  [fused_device(): return (split, scale[0].T, scale[1].T)]
    reduce_sum x3 -> x0, other arithmetic: 1.12 us -> none  [the longest x1 0.72 us: token_picker(): return jnp.sum(matches.reshape(matches.shape[0], seq_count, TOPK), axis=2)]
    reshape x3 -> x2, local copies, waits for them, and re-layouts: 3.07 us -> 3.52 us  [the longest x1 2.26 us: fused_device(): split = jnp.swapaxes(dispatched.reshape(CAP, experts_local, -1), 0, 1)]
where the time goes in v2:
time: 72 us; the launch traced here: 71.8 us
  Pallas kernels  65.5 us (91%)
  local copies, waits for them, and re-layouts  5.63 us (8%)
    pallas_call x1, Pallas kernels, fused_device(): pl.pallas_call(functools.partial(step_kernel, zs, chunks), out_shape=(jax...  65.5 us
    reshape x1, local copies, waits for them, and re-layouts, fused_device(): split = jnp.swapaxes(dispatched.reshape(CAP, experts_local, -1), 0, 1)  2.26 us

profile of v2, /device:TPU:1, one launch (start us, length us, event | category | flops | bytes accessed | tf_op | source)
XLA Modules:
  0.0 71.8 jit_solution(13631074742812542592)
XLA Ops:
  0.6 1.3 %reshape.20.gain_ref = bf16[1,448]{1,0:T(2,128)(2,1)} reshape(bf16[448]{0:T(512)(128)(2,1)} %param.15) | data formatting | bytes 1792 | tf_op jit(solution)/shard_map/reshape | solution.py:646
  1.9 65.5 %shard_map.112 = (bf16[32,7168]{1,0:T(8,128)(2,1)}, f32[8,128]{1,0:T(8,128)}) custom-call(bf16[5,8,1152]{2,1,0:T(8,128)(2,1)} %bitcast.13, bf16[40,576,128]{2,1,0:T(8,128)(2,1)} %bitcast.10, s32[40]{0:T(128)} %ctx_ref.1, bf16[1024,128]{1,0:T(8,128)(2,1)} %up_ref.1, bf16[256,7168]{1,0:T(8,128)(2,1)} %proj_hbm.1, bf16[40,448]{1,0:T(8,128)(2,1)} %resid_ref.1, ...), custom_call_target="tpu_custom_call" | custom-call | tf_op jit(solution)/shard_map/pallas_call | solution.py:587
  67.4 0.8 %slice_reduce_fusion = (f32[32]{0:T(128)S(1)}, f32[32]{0:T(128)S(1)}) fusion(f32[8,128]{1,0:T(8,128)} %get-tuple-element.6), kind=kLoop, calls=%fused_computation.1 | loop fusion | bytes 512 | tf_op jit(solution)/shard_map/slice | solution.py:652
  68.2 0.6 squeeze.6
  68.9 0.6 squeeze.7
  69.5 2.3 %copy.14 = bf16[2,16,7168]{2,0,1:T(2,128)(2,1)} copy(bf16[2,16,7168]{2,1,0:T(8,128)(2,1)} %bitcast.12) | data formatting | bytes 917504 | tf_op jit(solution)/shard_map/reshape | solution.py:650

commit v3 on v2

--- a/solution.py
+++ b/solution.py
@@ -135,6 +135,7 @@
 LINKED_Y = 2
 LANES = 128
 ROWS = 8
+GROUP = 2
 F32 = jnp.float32
 BF16 = jnp.bfloat16
 
@@ -205,7 +206,6 @@
     out_ref,
     scale_ref,
     qown,
-    gainown,
     pick_scr,
     cache,
     proj,
@@ -220,7 +220,7 @@
     k2,
     r3,
     merged,
-    part,
+    mine,
     ps1,
     pr1,
     pk1,
@@ -228,7 +228,8 @@
     pk2,
     pr3,
     gbuf,
-    gainbuf,
+    codes,
+    peaks,
     load_sem,
     proj_sem,
     qz_s,
@@ -285,18 +286,6 @@
         axis=-1,
     ).astype(BF16)
 
-    def placed(block):
-        zero = jnp.zeros_like(block)
-        return jnp.where(
-            core == 0,
-            jnp.concatenate([block, zero], axis=-1),
-            jnp.concatenate([zero, block], axis=-1),
-        )
-
-    gainown[...] = placed(
-        jnp.broadcast_to(gain_ref[...].astype(F32), (ROWS, gain_ref.shape[-1]))
-    ).astype(BF16)
-
     ids, gates = ids_ref[...], gates_ref[...]
     slots, seqs = out_ref.shape[0], ids.shape[1]
     experts = slots // CAP
@@ -338,9 +327,6 @@
             pending.append(one)
         return made
 
-    gain_copy = launch(
-        [copy(gainown, gainbuf, p_s.at[4], p_r.at[4], partner)]
-    )
     q_along = [
         launch(z_copies(lambda zz: qown.at[k], qbuf.at[k, core, y, z], qz_s.at[k], qz_r.at[k]))
         for k in range(chunks)
@@ -440,112 +426,148 @@
         for head, (out, _, total) in enumerate(merge(blocks)):
             merged[head, pl.ds(k * ROWS, ROWS), :] = out / total
 
-    for t in range(chunks + 5):
-        for stage, lag in (
-            (gather_across, 0),
-            (gather_pair, 1),
-            (attend, 2),
-            (merge_pair, 3),
-            (merge_across, 4),
-            (merge_along, 5),
-        ):
+    cols = resid_ref.shape[-1]
+    chip_cols = cols * CORES
+    p_pair, p_across, p_along, g_along, g_across, g_pair = {}, {}, {}, {}, {}, {}
+
+    def span(g):
+        first = g * GROUP
+        return first, min(GROUP, chunks - first)
+
+    def project(g):
+        first, size = span(g)
+        values = []
+        for head in range(2):
+            own = merged[head, pl.ds(first * ROWS, size * ROWS), :]
+            high = own.astype(BF16)
+            low = (own - high.astype(F32)).astype(BF16)
+            rows = up_ref[head * LAT : (head + 1) * LAT]
+            values.append(
+                jnp.dot(high, rows, preferred_element_type=F32)
+                + jnp.dot(low, rows, preferred_element_type=F32)
+            )
+        value = jnp.concatenate(values, axis=1).astype(BF16)
+        if g == 0:
+            proj_load.wait()
+        here = pl.ds(first, size)
+        for zz in range(zs):
+            for yy in range(LINKED_Y):
+                start = (zz * LINKED_Y + yy) * chip_cols
+                both = jnp.dot(
+                    value, proj[:, start : start + chip_cols], preferred_element_type=F32
+                ).reshape(size, ROWS, chip_cols)
+                low, high = both[..., :cols], both[..., cols:]
+                mine[here, yy, zz] = jnp.where(core == 0, low, high)
+                ps1[here, yy, zz] = jnp.where(core == 0, high, low).astype(BF16)
+        p_pair[g] = launch([copy(ps1.at[here], pr1.at[here], p_s.at[g, 0], p_r.at[g, 0], partner)])
+
+    def sum_pair(g):
+        here = pl.ds(*span(g))
+        p_pair[g][0].wait_recv()
+        pk1[here] = (mine[here, 1 - y] + pr1[here, 1 - y].astype(F32)).astype(BF16)
+        p_across[g] = launch([copy(pk1.at[here], pr2.at[here], p_s.at[g, 1], p_r.at[g, 1], across)])
+
+    def sum_across(g):
+        here = pl.ds(*span(g))
+        p_across[g][0].wait_recv()
+        kept = mine[here, y] + pr1[here, y].astype(F32) + pr2[here].astype(F32)
+        mine[here, y] = kept
+        pk2[here] = kept.astype(BF16)
+        p_along[g] = launch(
+            [
+                copy(
+                    pk2.at[here, zz],
+                    pr3.at[step, here],
+                    pz_s.at[g, 0, step],
+                    pz_r.at[g, 0, step],
+                    device(zz, y, core),
+                )
+                for step, zz in enumerate(along)
+            ]
+        )
+
+    def sum_along(g):
+        here = pl.ds(*span(g))
+        for one in p_along[g]:
+            one.wait_recv()
+        summed = mine[here, y, z] + resid_ref[here].astype(F32)
+        for step in range(zs - 1):
+            summed = summed + pr3[step, here].astype(F32)
+        scaled = summed * gain_ref[...].astype(F32)
+        square = jnp.sum(summed * summed, axis=-1, keepdims=True)
+        largest = jnp.max(jnp.abs(scaled), axis=-1, keepdims=True)
+        shape = summed.shape[:-1] + (gbuf.shape[-1] - cols,)
+        stats = put_lanes(shape, list(enumerate(split3(square) + split3(largest))))
+        gbuf[here, core, y, z] = jnp.concatenate([scaled, stats], axis=-1).astype(BF16)
+        block = gbuf.at[here, core, y, z]
+        g_along[g] = launch(
+            [
+                copy(block, block, pz_s.at[g, 1, step], pz_r.at[g, 1, step], device(zz, y, core))
+                for step, zz in enumerate(along)
+            ]
+        )
+
+    def spread_across(g):
+        here = pl.ds(*span(g))
+        for one in g_along[g]:
+            one.wait_recv()
+        block = gbuf.at[here, core, y]
+        g_across[g] = launch([copy(block, block, p_s.at[g, 2], p_r.at[g, 2], across)])
+
+    def spread_pair(g):
+        here = pl.ds(*span(g))
+        g_across[g][0].wait_recv()
+        block = gbuf.at[here, core]
+        g_pair[g] = launch([copy(block, block, p_s.at[g, 3], p_r.at[g, 3], partner)])
+
+    def finish(g):
+        first, size = span(g)
+        g_pair[g][0].wait_recv()
+        for k in range(first, first + size):
+            here = pl.ds(k * ROWS, ROWS)
+            stats = gbuf[k, :, :, :, :, cols:].astype(F32).reshape(count, ROWS, -1)
+            square = jnp.sum(take3(stats, 0), axis=0)
+            largest = jnp.max(take3(stats, 3), axis=0)
+            inverse = lax.rsqrt(square / (chip_cols * LINKED_Y * zs) + small_eps)
+            peak = largest * inverse + small_eps
+            factor = inverse / peak
+            peaks[here] = jnp.broadcast_to(peak, (ROWS, LANES))
+            for zz in range(zs):
+                for yy in range(LINKED_Y):
+                    start = (zz * LINKED_Y + yy) * chip_cols
+                    rows = [gbuf[k, cc, yy, zz, :, :cols].astype(F32) for cc in range(CORES)]
+                    codes[here, start : start + chip_cols] = (
+                        jnp.concatenate(rows, axis=1) * factor
+                    ).astype(BF16)
+
+    chunk_stages = (gather_across, gather_pair, attend, merge_pair, merge_across, merge_along)
+    group_stages = (
+        project,
+        sum_pair,
+        sum_across,
+        sum_along,
+        spread_across,
+        spread_pair,
+        finish,
+    )
+    groups = -(-chunks // GROUP)
+    for t in range(chunks + len(chunk_stages) + len(group_stages)):
+        for lag, stage in enumerate(chunk_stages):
             if 0 <= t - lag < chunks:
                 stage(t - lag)
-
-    values = []
-    for head in range(2):
-        own = merged[head]
-        high = own.astype(BF16)
-        low = (own - high.astype(F32)).astype(BF16)
-        rows = up_ref[head * LAT : (head + 1) * LAT]
-        values.append(
-            jnp.dot(high, rows, preferred_element_type=F32)
-            + jnp.dot(low, rows, preferred_element_type=F32)
-        )
-    value = jnp.concatenate(values, axis=1).astype(BF16)
-    proj_load.wait()
-    chip_cols = part.shape[-1]
-    held = ps1.shape[-1]
-    skip = chip_cols - held
-    for zz in range(zs):
-        for yy in range(LINKED_Y):
-            start = (zz * LINKED_Y + yy) * chip_cols
-            part[yy, zz] = jnp.dot(
-                value, proj[:, start : start + chip_cols], preferred_element_type=F32
-            )
-    part[y, z] = part[y, z] + placed(resid_ref[...].astype(F32))
-    own_cols = pl.ds(pl.multiple_of(core * skip, LANES), held)
-    other_cols = pl.ds(pl.multiple_of((1 - core) * skip, LANES), held)
-    ps1[...] = part[:, :, :, other_cols].astype(BF16)
-    p_pair = launch([copy(ps1, pr1, p_s.at[0], p_r.at[0], partner)])
-    p_pair[0].wait_recv()
-    pk1[...] = (part[1 - y, :, :, own_cols] + pr1[1 - y].astype(F32)).astype(BF16)
-    p_across = launch([copy(pk1, pr2, p_s.at[1], p_r.at[1], across)])
-    p_across[0].wait_recv()
-    kept = part[y, :, :, own_cols] + pr1[y].astype(F32) + pr2[...].astype(F32)
-    part[y, :, :, own_cols] = kept
-    pk2[...] = kept.astype(BF16)
-    p_along = launch(
-        [
-            copy(pk2.at[zz], pr3.at[step], pz_s.at[0, step], pz_r.at[0, step], device(zz, y, core))
-            for step, zz in enumerate(along)
-        ]
-    )
-    gain_copy[0].wait_recv()
-    for one in p_along:
-        one.wait_recv()
-    summed = part[y, z, :, own_cols]
-    for step in range(zs - 1):
-        summed = summed + pr3[step].astype(F32)
-    gain = (gainown[...].astype(F32) + gainbuf[...].astype(F32))[:1]
-    gain = jnp.where(core == 0, gain[:, :held], gain[:, skip:])
-    scaled = summed * gain
-    lane = lax.broadcasted_iota(jnp.int32, summed.shape, 1)
-    first = jnp.where(core == 0, 0, 2 * held - chip_cols)
-    square = jnp.sum(jnp.where(lane >= first, summed * summed, 0.0), axis=1, keepdims=True)
-    largest = jnp.max(jnp.abs(scaled), axis=1, keepdims=True)
-    columns = list(enumerate(split3(square) + split3(largest)))
-    stats = put_lanes((summed.shape[0], LANES), columns)
-    gbuf[core, y, z] = jnp.concatenate([scaled, stats], axis=1).astype(BF16)
-    g_along = launch(
-        [
-            copy(
-                gbuf.at[core, y, z],
-                gbuf.at[core, y, z],
-                pz_s.at[1, step],
-                pz_r.at[1, step],
-                device(zz, y, core),
-            )
-            for step, zz in enumerate(along)
-        ]
-    )
-    for one in g_along:
-        one.wait_recv()
-    g_across = launch([copy(gbuf.at[core, y], gbuf.at[core, y], p_s.at[2], p_r.at[2], across)])
-    g_across[0].wait_recv()
-    g_pair = launch([copy(gbuf.at[core], gbuf.at[core], p_s.at[3], p_r.at[3], partner)])
-    g_pair[0].wait_recv()
-
-    stats = gbuf[:, :, :, :, held:].astype(F32).reshape(count, summed.shape[0], LANES)
-    square = jnp.sum(take3(stats, 0), axis=0)
-    largest = jnp.max(take3(stats, 3), axis=0)
-    inverse = lax.rsqrt(square / (chip_cols * LINKED_Y * zs) + small_eps)
-    peak = largest * inverse + small_eps
-    factor = inverse / peak
+        for lag, stage in enumerate(group_stages):
+            for g in range(groups):
+                if sum(span(g)) - 1 + len(chunk_stages) - 1 + lag == t:
+                    stage(g)
+
     pick = pick_scr[...].astype(BF16)
-    for zz in range(zs):
-        for yy in range(LINKED_Y):
-            start = (zz * LINKED_Y + yy) * chip_cols
-            for cc in range(CORES):
-                drop = cc * (2 * held - chip_cols)
-                rows = gbuf[cc, yy, zz, :, drop:held].astype(F32) * factor
-                at = start + cc * held
-                out_ref[:, at : at + held - drop] = jnp.dot(
-                    pick, rows.astype(BF16), preferred_element_type=F32
-                ).astype(BF16)
+    for start in range(0, codes.shape[1], chip_cols):
+        out_ref[:, start : start + chip_cols] = jnp.dot(
+            pick, codes[:, start : start + chip_cols], preferred_element_type=F32
+        ).astype(BF16)
     scales = jnp.dot(
         pick_scr[...],
-        jnp.broadcast_to(peak, (peak.shape[0], LANES)),
+        peaks[...],
         precision=lax.Precision.HIGHEST,
         preferred_element_type=F32,
     )
@@ -576,7 +598,8 @@
     width = queries.shape[1]
     cols = residual.shape[1]
     chip_cols = cols * CORES
-    held = -(-cols // LANES) * LANES
+    held = -(-(cols + 6) // LANES) * LANES
+    groups = -(-chunks // GROUP)
     experts_local = EXPERTS // kv_count
     slot_count = experts_local * CAP
     vmem = pl.BlockSpec(memory_space=pltpu.VMEM)
@@ -594,7 +617,6 @@
         out_specs=(vmem, vmem),
         scratch_shapes=[
             pltpu.VMEM((chunks, ROWS, width), BF16),
-            pltpu.VMEM((ROWS, chip_cols), BF16),
             pltpu.VMEM((slot_count, seq_count), F32),
             pltpu.VMEM((seq_count, LAT + ROPE, ctx_local), BF16),
             pltpu.VMEM(out_proj.shape, BF16),
@@ -609,15 +631,16 @@
             pltpu.VMEM((chunks, zs, ROWS, width), BF16),
             pltpu.VMEM((chunks, zs - 1, ROWS, width), BF16),
             pltpu.VMEM((H // kv_count, seq_count, LAT), F32),
-            pltpu.VMEM(full + (seq_count, chip_cols), F32),
-            pltpu.VMEM(full + (seq_count, held), BF16),
-            pltpu.VMEM(full + (seq_count, held), BF16),
-            pltpu.VMEM((zs, seq_count, held), BF16),
-            pltpu.VMEM((zs, seq_count, held), BF16),
-            pltpu.VMEM((zs, seq_count, held), BF16),
-            pltpu.VMEM((zs - 1, seq_count, held), BF16),
-            pltpu.VMEM((CORES,) + full + (seq_count, held + LANES), BF16),
-            pltpu.VMEM((ROWS, chip_cols), BF16),
+            pltpu.VMEM((chunks,) + full + (ROWS, cols), F32),
+            pltpu.VMEM((chunks,) + full + (ROWS, cols), BF16),
+            pltpu.VMEM((chunks,) + full + (ROWS, cols), BF16),
+            pltpu.VMEM((chunks, zs, ROWS, cols), BF16),
+            pltpu.VMEM((chunks, zs, ROWS, cols), BF16),
+            pltpu.VMEM((chunks, zs, ROWS, cols), BF16),
+            pltpu.VMEM((zs - 1, chunks, ROWS, cols), BF16),
+            pltpu.VMEM((chunks, CORES) + full + (ROWS, held), BF16),
+            pltpu.VMEM((seq_count, chip_cols * LINKED_Y * zs), BF16),
+            pltpu.VMEM((seq_count, LANES), F32),
             dma((chunks,)),
             dma,
             dma((chunks, zs - 1)),
@@ -628,10 +651,10 @@
             dma((chunks, zs - 1)),
             dma((chunks, 2)),
             dma((chunks, 2)),
-            dma((2, zs - 1)),
-            dma((2, zs - 1)),
-            dma((5,)),
-            dma((5,)),
+            dma((groups, 2, zs - 1)),
+            dma((groups, 2, zs - 1)),
+            dma((groups, 4)),
+            dma((groups, 4)),
         ],
         compiler_params=pltpu.CompilerParams(
             collective_id=0, has_side_effects=True, vmem_limit_bytes=60 * 1024 * 1024
@@ -642,7 +665,7 @@
         context_lengths,
         value_up,
         out_proj,
-        residual,
+        residual.reshape(chunks, ROWS, cols),
         norm_gain.reshape(1, -1),
         expert_ids.T,
         gate_weights.T,

time: 72 us -> 66 us (0.917)
  Pallas kernels: 65.5 us -> 59.5 us
    pallas_call x1, Pallas kernels: 65.5 us -> 59.5 us  [fused_device(): pl.pallas_call(functools.partial(step_kernel, zs, chunks), out_shape=(jax...]
where the time goes in v3:
time: 66 us; the launch traced here: 65.8 us
  Pallas kernels  59.5 us (90%)
  local copies, waits for them, and re-layouts  5.63 us (9%)
    pallas_call x1, Pallas kernels, fused_device(): pl.pallas_call(functools.partial(step_kernel, zs, chunks), out_shape=(jax...  59.5 us
    reshape x1, local copies, waits for them, and re-layouts, fused_device(): split = jnp.swapaxes(dispatched.reshape(CAP, experts_local, -1), 0, 1)  2.26 us

profile of v3, /device:TPU:1, one launch (start us, length us, event | category | flops | bytes accessed | tf_op | source)
XLA Modules:
  0.0 65.8 jit_solution(16946938698840113869)
XLA Ops:
  0.6 1.3 %reshape.24.gain_ref = bf16[1,448]{1,0:T(2,128)(2,1)} reshape(bf16[448]{0:T(512)(128)(2,1)} %param.15) | data formatting | bytes 1792 | tf_op jit(solution)/shard_map/reshape | solution.py:669
  1.9 59.5 %shard_map.112 = (bf16[32,7168]{1,0:T(8,128)(2,1)}, f32[8,128]{1,0:T(8,128)}) custom-call(bf16[5,8,1152]{2,1,0:T(8,128)(2,1)} %bitcast.14, bf16[40,576,128]{2,1,0:T(8,128)(2,1)} %bitcast.11, s32[40]{0:T(128)} %ctx_ref.1, bf16[1024,128]{1,0:T(8,128)(2,1)} %up_ref.1, bf16[256,7168]{1,0:T(8,128)(2,1)} %proj_hbm.1, bf16[5,8,448]{2,1,0:T(8,128)(2,1)} %bitcast.15, ...), custom_call_target="tpu_custom_call" | custom-call | tf_op jit(solution)/shard_map/pallas_call | solution.py:610
  61.4 0.8 %slice_reduce_fusion = (f32[32]{0:T(128)S(1)}, f32[32]{0:T(128)S(1)}) fusion(f32[8,128]{1,0:T(8,128)} %get-tuple-element.6), kind=kLoop, calls=%fused_computation.1 | loop fusion | bytes 512 | tf_op jit(solution)/shard_map/slice | solution.py:675
  62.3 0.6 squeeze.6
  62.9 0.6 squeeze.7
  63.5 2.3 %copy.14 = bf16[2,16,7168]{2,0,1:T(2,128)(2,1)} copy(bf16[2,16,7168]{2,1,0:T(8,128)(2,1)} %bitcast.13) | data formatting | bytes 917504 | tf_op jit(solution)/shard_map/reshape | solution.py:673

commit v4 on v3

--- a/solution.py
+++ b/solution.py
@@ -136,6 +136,7 @@
 LANES = 128
 ROWS = 8
 GROUP = 2
+LAGS = (0, 2, 3, 5, 8, 11, 11, 13, 15, 18, 20, 22, 23)
 F32 = jnp.float32
 BF16 = jnp.bfloat16
 
@@ -205,6 +206,7 @@
     gates_ref,
     out_ref,
     scale_ref,
+    gate_ref,
     qown,
     pick_scr,
     cache,
@@ -287,23 +289,27 @@
     ).astype(BF16)
 
     ids, gates = ids_ref[...], gates_ref[...]
-    slots, seqs = out_ref.shape[0], ids.shape[1]
-    experts = slots // CAP
-    expert = me * experts + lax.broadcasted_iota(jnp.int32, (experts, seqs), 0)
-    member, gate = jnp.zeros((experts, seqs), F32), jnp.zeros((experts, seqs), F32)
-    for choice in range(ids.shape[0]):
-        same = ids[choice : choice + 1] == expert
-        member = jnp.where(same, 1.0, member)
-        gate = jnp.where(same, gates[choice : choice + 1], gate)
+    experts, seqs = out_ref.shape[0], ids.shape[1]
+    slots = experts * CAP
     earlier = lax.broadcasted_iota(jnp.int32, (seqs, seqs), 0) < lax.broadcasted_iota(
         jnp.int32, (seqs, seqs), 1
     )
-    rank = jnp.dot(
-        member.astype(BF16), earlier.astype(F32).astype(BF16), preferred_element_type=F32
-    )
-    picks = [jnp.where(jnp.abs(rank - slot) < 0.5, member, 0.0) for slot in range(CAP)]
-    pick_scr[...] = jnp.concatenate(picks, axis=0)
-    slot_gates = [jnp.sum(pick * gate, axis=1, keepdims=True) for pick in picks]
+    earlier = earlier.astype(F32).astype(BF16)
+    line = lax.broadcasted_iota(jnp.int32, (slots, seqs), 0)
+
+    def choose(expert, slot):
+        member, gate = jnp.zeros((slots, seqs), F32), jnp.zeros((slots, seqs), F32)
+        for choice in range(ids.shape[0]):
+            same = ids[choice : choice + 1] == me * experts + expert
+            member = jnp.where(same, 1.0, member)
+            gate = jnp.where(same, gates[choice : choice + 1], gate)
+        rank = jnp.dot(member.astype(BF16), earlier, preferred_element_type=F32)
+        return jnp.where(jnp.abs(rank - slot.astype(F32)) < 0.5, member, 0.0), gate
+
+    pick_scr[0] = choose(line // CAP, lax.rem(line, CAP))[0]
+    by_slot, gate = choose(lax.rem(line, experts), line // experts)
+    pick_scr[1] = by_slot
+    slot_gates = jnp.sum(by_slot * gate, axis=1, keepdims=True)
 
     barrier = pltpu.get_barrier_semaphore()
     peers = [partner, across] + [device(zz, y, core) for zz in along]
@@ -551,30 +557,33 @@
         finish,
     )
     groups = -(-chunks // GROUP)
-    for t in range(chunks + len(chunk_stages) + len(group_stages)):
-        for lag, stage in enumerate(chunk_stages):
-            if 0 <= t - lag < chunks:
-                stage(t - lag)
-        for lag, stage in enumerate(group_stages):
-            for g in range(groups):
-                if sum(span(g)) - 1 + len(chunk_stages) - 1 + lag == t:
-                    stage(g)
-
-    pick = pick_scr[...].astype(BF16)
+    order = []
+    for rank, stage in enumerate(chunk_stages):
+        for k in range(chunks):
+            order.append((k + LAGS[rank], rank, stage, k))
+    for rank, stage in enumerate(group_stages, len(chunk_stages)):
+        for g in range(groups):
+            order.append((sum(span(g)) - 1 + LAGS[rank], rank, stage, g))
+    for _, _, stage, index in sorted(order, key=lambda entry: entry[:2]):
+        stage(index)
+
+    pick = pick_scr[0].astype(BF16)
     for start in range(0, codes.shape[1], chip_cols):
-        out_ref[:, start : start + chip_cols] = jnp.dot(
-            pick, codes[:, start : start + chip_cols], preferred_element_type=F32
-        ).astype(BF16)
+        out_ref[:, :, start : start + chip_cols] = (
+            jnp.dot(pick, codes[:, start : start + chip_cols], preferred_element_type=F32)
+            .reshape(experts, CAP, chip_cols)
+            .astype(BF16)
+        )
     scales = jnp.dot(
-        pick_scr[...],
-        peaks[...],
-        precision=lax.Precision.HIGHEST,
-        preferred_element_type=F32,
-    )
-    wide = jnp.broadcast_to(jnp.concatenate(slot_gates, axis=0), (slots, LANES))
+        pick_scr[1], peaks[...], precision=lax.Precision.HIGHEST, preferred_element_type=F32
+    )
+    wide = jnp.broadcast_to(slot_gates, (slots, LANES))
     tail = jnp.zeros((LANES - 2 * slots, LANES), F32)
-    flat = jnp.transpose(jnp.concatenate([scales, wide, tail], axis=0))
-    scale_ref[...] = flat[:ROWS]
+    flat = jnp.transpose(jnp.concatenate([scales, wide, tail], axis=0))[:1]
+    for slot in range(CAP):
+        at = slot * experts
+        scale_ref[slot : slot + 1] = flat[:, at : at + experts]
+        gate_ref[slot : slot + 1] = flat[:, slots + at : slots + at + experts]
     for one in pending:
         one.wait_send()
 
@@ -607,17 +616,18 @@
     anywhere = pl.BlockSpec(memory_space=pl.ANY)
     dma = pltpu.SemaphoreType.DMA
     full = (LINKED_Y, zs)
-    dispatched, scale = pl.pallas_call(
+    dispatched, scale, gate = pl.pallas_call(
         functools.partial(step_kernel, zs, chunks),
         out_shape=(
-            jax.ShapeDtypeStruct((slot_count, chip_cols * LINKED_Y * zs), BF16),
-            jax.ShapeDtypeStruct((ROWS, LANES), F32),
+            jax.ShapeDtypeStruct((experts_local, CAP, chip_cols * LINKED_Y * zs), BF16),
+            jax.ShapeDtypeStruct((CAP, experts_local), F32),
+            jax.ShapeDtypeStruct((CAP, experts_local), F32),
         ),
         in_specs=[vmem, anywhere, smem, vmem, anywhere, vmem, vmem, vmem, vmem],
-        out_specs=(vmem, vmem),
+        out_specs=(vmem, vmem, vmem),
         scratch_shapes=[
             pltpu.VMEM((chunks, ROWS, width), BF16),
-            pltpu.VMEM((slot_count, seq_count), F32),
+            pltpu.VMEM((2, slot_count, seq_count), F32),
             pltpu.VMEM((seq_count, LAT + ROPE, ctx_local), BF16),
             pltpu.VMEM(out_proj.shape, BF16),
             pltpu.VMEM((chunks, CORES) + full + (ROWS, width), BF16),
@@ -670,9 +680,7 @@
         expert_ids.T,
         gate_weights.T,
     )
-    split = jnp.swapaxes(dispatched.reshape(CAP, experts_local, -1), 0, 1)
-    scale = scale[0].reshape(-1, CAP, experts_local)
-    return split, scale[0].T, scale[1].T
+    return dispatched, scale.T, gate.T
 
 
 def per_device(*arrays):

time: 66 us -> 63.6 us (0.964)
  Pallas kernels: 59.5 us -> 56.9 us
    unnamed x0 -> x3, local copies, waits for them, and re-layouts: none -> 4.56 us
    pallas_call x1, Pallas kernels: 59.5 us -> 56.9 us  [fused_device(): pl.pallas_call(functools.partial(step_kernel, zs, chunks), out_shape=(jax...]
    reshape x1 -> x0, local copies, waits for them, and re-layouts: 2.26 us -> none  [fused_device(): split = jnp.swapaxes(dispatched.reshape(CAP, experts_local, -1), 0, 1)]
    squeeze x2 -> x0, local copies, waits for them, and re-layouts: 1.28 us -> none  [fused_device(): return (split, scale[0].T, scale[1].T)]
    slice x1 -> x0, local copies, waits for them, and re-layouts: 0.84 us -> none  [fused_device(): return (split, scale[0].T, scale[1].T)]
where the time goes in v4:
time: 63.6 us; the launch traced here: 63.4 us
  Pallas kernels  56.9 us (89%)
  local copies, waits for them, and re-layouts  5.82 us (9%)
  between operations  0.64 us (1%)
    pallas_call x1, Pallas kernels, fused_device(): pl.pallas_call(functools.partial(step_kernel, zs, chunks), out_shape=(jax...  56.9 us
    unnamed x3, local copies, waits for them, and re-layouts  4.56 us

profile of v4, /device:TPU:1, one launch (start us, length us, event | category | flops | bytes accessed | tf_op | source)
XLA Modules:
  0.0 63.4 jit_solution(6570783681461109182)
XLA Ops:
  0.6 1.3 %reshape.17.gain_ref = bf16[1,448]{1,0:T(2,128)(2,1)} reshape(bf16[448]{0:T(512)(128)(2,1)} %param.15) | data formatting | bytes 1792 | tf_op jit(solution)/shard_map/reshape | solution.py:679
  1.9 56.9 %shard_map.112 = (bf16[16,2,7168]{2,1,0:T(2,128)(2,1)}, f32[2,16]{1,0:T(2,128)}, f32[2,16]{1,0:T(2,128)}) custom-call(bf16[5,8,1152]{2,1,0:T(8,128)(2,1)} %bitcast.8, bf16[40,576,128]{2,1,0:T(8,128)(2,1)} %bitcast.7, s32[40]{0:T(128)} %ctx_ref.1, bf16[1024,128]{1,0:T(8,128)(2,1)} %up_ref.1, bf16[256,7168]{1,0:T(8,128)(2,1)} %proj_hbm.1, ...), custom_call_target="tpu_custom_call" | custom-call | tf_op jit(solution)/shard_map/pallas_call | solution.py:619
  58.8 2.1 %copy.15 = bf16[16,2,7168]{2,1,0:T(2,128)(2,1)} copy(bf16[16,2,7168]{2,1,0:T(2,128)(2,1)} %get-tuple-element.12) | data formatting | bytes 917504
  60.9 1.2 %copy.16 = f32[16,2]{0,1:T(2,128)} copy(f32[16,2]{0,1:T(2,128)} %bitcast.13) | data formatting | bytes 256
  62.2 1.2 %copy.17 = f32[16,2]{0,1:T(2,128)} copy(f32[16,2]{0,1:T(2,128)} %bitcast.12) | data formatting | bytes 256

commit v5 on v4

--- a/solution.py
+++ b/solution.py
@@ -135,8 +135,8 @@
 LINKED_Y = 2
 LANES = 128
 ROWS = 8
-GROUP = 2
-LAGS = (0, 2, 3, 5, 8, 11, 11, 13, 15, 18, 20, 22, 23)
+GROUP = 1
+LAGS = (0, 2, 3, 4.5, 8, 12, 12, 13, 15, 18, 20, 22, 23)
 F32 = jnp.float32
 BF16 = jnp.bfloat16
 
@@ -202,13 +202,9 @@
     proj_hbm,
     resid_ref,
     gain_ref,
-    ids_ref,
-    gates_ref,
-    out_ref,
-    scale_ref,
-    gate_ref,
+    codes,
+    peaks,
     qown,
-    pick_scr,
     cache,
     proj,
     qbuf,
@@ -230,8 +226,6 @@
     pk2,
     pr3,
     gbuf,
-    codes,
-    peaks,
     load_sem,
     proj_sem,
     qz_s,
@@ -287,29 +281,6 @@
         [raw[..., :LAT], raw[..., key : key + LAT], raw[..., LAT:key], raw[..., key + LAT :]],
         axis=-1,
     ).astype(BF16)
-
-    ids, gates = ids_ref[...], gates_ref[...]
-    experts, seqs = out_ref.shape[0], ids.shape[1]
-    slots = experts * CAP
-    earlier = lax.broadcasted_iota(jnp.int32, (seqs, seqs), 0) < lax.broadcasted_iota(
-        jnp.int32, (seqs, seqs), 1
-    )
-    earlier = earlier.astype(F32).astype(BF16)
-    line = lax.broadcasted_iota(jnp.int32, (slots, seqs), 0)
-
-    def choose(expert, slot):
-        member, gate = jnp.zeros((slots, seqs), F32), jnp.zeros((slots, seqs), F32)
-        for choice in range(ids.shape[0]):
-            same = ids[choice : choice + 1] == me * experts + expert
-            member = jnp.where(same, 1.0, member)
-            gate = jnp.where(same, gates[choice : choice + 1], gate)
-        rank = jnp.dot(member.astype(BF16), earlier, preferred_element_type=F32)
-        return jnp.where(jnp.abs(rank - slot.astype(F32)) < 0.5, member, 0.0), gate
-
-    pick_scr[0] = choose(line // CAP, lax.rem(line, CAP))[0]
-    by_slot, gate = choose(lax.rem(line, experts), line // experts)
-    pick_scr[1] = by_slot
-    slot_gates = jnp.sum(by_slot * gate, axis=1, keepdims=True)
 
     barrier = pltpu.get_barrier_semaphore()
     peers = [partner, across] + [device(zz, y, core) for zz in along]
@@ -567,15 +538,42 @@
     for _, _, stage, index in sorted(order, key=lambda entry: entry[:2]):
         stage(index)
 
-    pick = pick_scr[0].astype(BF16)
-    for start in range(0, codes.shape[1], chip_cols):
-        out_ref[:, :, start : start + chip_cols] = (
-            jnp.dot(pick, codes[:, start : start + chip_cols], preferred_element_type=F32)
-            .reshape(experts, CAP, chip_cols)
+    for one in pending:
+        one.wait_send()
+
+
+def dispatch_kernel(width, codes, peaks, ids_ref, gates_ref, out_ref, scale_ref, gate_ref):
+    me = lax.axis_index("kv")
+    ids, gates = ids_ref[...], gates_ref[...]
+    experts, seqs = out_ref.shape[0], ids.shape[1]
+    slots = experts * CAP
+    earlier = lax.broadcasted_iota(jnp.int32, (seqs, seqs), 0) < lax.broadcasted_iota(
+        jnp.int32, (seqs, seqs), 1
+    )
+    earlier = earlier.astype(F32).astype(BF16)
+    line = lax.broadcasted_iota(jnp.int32, (slots, seqs), 0)
+
+    def choose(expert, slot):
+        member, gate = jnp.zeros((slots, seqs), F32), jnp.zeros((slots, seqs), F32)
+        for choice in range(ids.shape[0]):
+            same = ids[choice : choice + 1] == me * experts + expert
+            member = jnp.where(same, 1.0, member)
+            gate = jnp.where(same, gates[choice : choice + 1], gate)
+        rank = jnp.dot(member.astype(BF16), earlier, preferred_element_type=F32)
+        return jnp.where(jnp.abs(rank - slot.astype(F32)) < 0.5, member, 0.0), gate
+
+    pick = choose(line // CAP, lax.rem(line, CAP))[0].astype(BF16)
+    by_slot, gate = choose(lax.rem(line, experts), line // experts)
+    slot_gates = jnp.sum(by_slot * gate, axis=1, keepdims=True)
+
+    for start in range(0, codes.shape[1], width):
+        out_ref[:, :, start : start + width] = (
+            jnp.dot(pick, codes[:, start : start + width], preferred_element_type=F32)
+            .reshape(experts, CAP, width)
             .astype(BF16)
         )
     scales = jnp.dot(
-        pick_scr[1], peaks[...], precision=lax.Precision.HIGHEST, preferred_element_type=F32
+        by_slot, peaks[...], precision=lax.Precision.HIGHEST, preferred_element_type=F32
     )
     wide = jnp.broadcast_to(slot_gates, (slots, LANES))
     tail = jnp.zeros((LANES - 2 * slots, LANES), F32)
@@ -584,8 +582,6 @@
         at = slot * experts
         scale_ref[slot : slot + 1] = flat[:, at : at + experts]
         gate_ref[slot : slot + 1] = flat[:, slots + at : slots + at + experts]
-    for one in pending:
-        one.wait_send()
 
 
 def fused_device(
@@ -610,24 +606,21 @@
     held = -(-(cols + 6) // LANES) * LANES
     groups = -(-chunks // GROUP)
     experts_local = EXPERTS // kv_count
-    slot_count = experts_local * CAP
     vmem = pl.BlockSpec(memory_space=pltpu.VMEM)
     smem = pl.BlockSpec(memory_space=pltpu.SMEM)
     anywhere = pl.BlockSpec(memory_space=pl.ANY)
     dma = pltpu.SemaphoreType.DMA
     full = (LINKED_Y, zs)
-    dispatched, scale, gate = pl.pallas_call(
+    codes, peaks = pl.pallas_call(
         functools.partial(step_kernel, zs, chunks),
         out_shape=(
-            jax.ShapeDtypeStruct((experts_local, CAP, chip_cols * LINKED_Y * zs), BF16),
-            jax.ShapeDtypeStruct((CAP, experts_local), F32),
-            jax.ShapeDtypeStruct((CAP, experts_local), F32),
+            jax.ShapeDtypeStruct((seq_count, chip_cols * LINKED_Y * zs), BF16),
+            jax.ShapeDtypeStruct((seq_count, LANES), F32),
         ),
-        in_specs=[vmem, anywhere, smem, vmem, anywhere, vmem, vmem, vmem, vmem],
-        out_specs=(vmem, vmem, vmem),
+        in_specs=[vmem, anywhere, smem, vmem, anywhere, vmem, vmem],
+        out_specs=(vmem, vmem),
         scratch_shapes=[
             pltpu.VMEM((chunks, ROWS, width), BF16),
-            pltpu.VMEM((2, slot_count, seq_count), F32),
             pltpu.VMEM((seq_count, LAT + ROPE, ctx_local), BF16),
             pltpu.VMEM(out_proj.shape, BF16),
             pltpu.VMEM((chunks, CORES) + full + (ROWS, width), BF16),
@@ -649,8 +642,6 @@
             pltpu.VMEM((chunks, zs, ROWS, cols), BF16),
             pltpu.VMEM((zs - 1, chunks, ROWS, cols), BF16),
             pltpu.VMEM((chunks, CORES) + full + (ROWS, held), BF16),
-            pltpu.VMEM((seq_count, chip_cols * LINKED_Y * zs), BF16),
-            pltpu.VMEM((seq_count, LANES), F32),
             dma((chunks,)),
             dma,
             dma((chunks, zs - 1)),
@@ -677,9 +668,17 @@
         out_proj,
         residual.reshape(chunks, ROWS, cols),
         norm_gain.reshape(1, -1),
-        expert_ids.T,
-        gate_weights.T,
-    )
+    )
+    dispatched, scale, gate = pl.pallas_call(
+        functools.partial(dispatch_kernel, chip_cols),
+        out_shape=(
+            jax.ShapeDtypeStruct((experts_local, CAP, codes.shape[1]), BF16),
+            jax.ShapeDtypeStruct((CAP, experts_local), F32),
+            jax.ShapeDtypeStruct((CAP, experts_local), F32),
+        ),
+        in_specs=[vmem] * 4,
+        out_specs=(vmem, vmem, vmem),
+    )(codes, peaks, expert_ids.T, gate_weights.T)
     return dispatched, scale.T, gate.T
 
 

time: 63.6 us -> 58.9 us (0.926)
  local copies, waits for them, and re-layouts: 5.82 us -> 1.26 us
    unnamed x3 -> x0, local copies, waits for them, and re-layouts: 4.56 us -> none
    pallas_call x1, Pallas kernels: 56.9 us -> 54.2 us  [fused_device(): pl.pallas_call(functools.partial(step_kernel, zs, chunks), out_shape=(jax...]
    pallas_call x0 -> x1, Pallas kernels: none -> 2.62 us  [fused_device(): pl.pallas_call(functools.partial(dispatch_kernel, chip_cols), out_shape=(...]
where the time goes in v5:
time: 58.9 us; the launch traced here: 58.7 us
  Pallas kernels  56.8 us (96%)
  local copies, waits for them, and re-layouts  1.26 us (2%)
  between operations  0.64 us (1%)
    pallas_call x1, Pallas kernels, fused_device(): pl.pallas_call(functools.partial(step_kernel, zs, chunks), out_shape=(jax...  54.2 us
    pallas_call x1, Pallas kernels, fused_device(): pl.pallas_call(functools.partial(dispatch_kernel, chip_cols), out_shape=(...  2.62 us
    reshape x1, local copies, waits for them, and re-layouts, fused_device(): norm_gain.reshape(1, -1)  1.26 us

profile of v5, /device:TPU:1, one launch (start us, length us, event | category | flops | bytes accessed | tf_op | source)
XLA Modules:
  0.0 58.7 jit_solution(7673049176003759686)
XLA Ops:
  0.6 1.3 %reshape.17.gain_ref = bf16[1,448]{1,0:T(2,128)(2,1)} reshape(bf16[448]{0:T(512)(128)(2,1)} %param.15) | data formatting | bytes 1792 | tf_op jit(solution)/shard_map/reshape | solution.py:670
  1.9 54.2 %shard_map.112 = (bf16[40,7168]{1,0:T(8,128)(2,1)}, f32[40,128]{1,0:T(8,128)}) custom-call(bf16[5,8,1152]{2,1,0:T(8,128)(2,1)} %bitcast.8, bf16[40,576,128]{2,1,0:T(8,128)(2,1)} %bitcast.7, s32[40]{0:T(128)} %ctx_ref.1, bf16[1024,128]{1,0:T(8,128)(2,1)} %up_ref.1, bf16[256,7168]{1,0:T(8,128)(2,1)} %proj_hbm.1, bf16[5,8,448]{2,1,0:T(8,128)(2,1)} %bitcast.9, ...), custom_call_target="tpu_custom_call" | custom-call | tf_op jit(solution)/shard_map/pallas_call | solution.py:614
  56.1 2.6 %shard_map.113 = (bf16[16,2,7168]{2,1,0:T(2,128)(2,1)}, f32[2,16]{1,0:T(2,128)}, f32[2,16]{1,0:T(2,128)}) custom-call(bf16[40,7168]{1,0:T(8,128)(2,1)} %get-tuple-element.8.codes, f32[40,128]{1,0:T(8,128)} %get-tuple-element.9.peaks, s32[8,40]{1,0:T(8,128)} %bitcast.10, f32[8,40]{1,0:T(8,128)} %bitcast.11), custom_call_target="tpu_custom_call" | custom-call | tf_op jit(solution)/shard_map/pallas_call | solution.py:672
